TPU v7x, 32 devices: a whole 2x2x4 slice. The times are simulated.
32 devices in a mesh: seq: 4 (over y, x), fsdp: 8 (over z, core).
Axes of the slice: x: 2, y: 2, z: 4, core: 2. Of those that a mesh axis runs over, the one named last changes fastest.
Arguments:
- hidden_in: bfloat16 [8, 1024, 2048], P('fsdp', 'seq'), may hold values from -6 to 6
- cotangent: bfloat16 [8, 1024, 2048], P('fsdp', 'seq'), may hold values from -6 to 6
- block_table: int32 [4, 2], replicated, may hold values from 0 to 7, as said below
- first_gain: bfloat16 [2048], P('fsdp'), may hold values from 0.5 to 1.5
- first_bias: bfloat16 [2048], P('fsdp'), may hold values from -3 to 3
- qkv_weight: bfloat16 [2048, 6144], P('fsdp'), may hold values from -0.125 to 0.125
- qkv_bias: bfloat16 [6144], P('fsdp')
- out_weight: bfloat16 [2048, 2048], P('fsdp'), may hold values from -2 to 2
- second_gain: bfloat16 [2048], P('fsdp'), may hold values from 0.5 to 1.5
- second_bias: bfloat16 [2048], P('fsdp'), may hold values from -3 to 3
- gate_weight: bfloat16 [2048, 5632], P('fsdp'), may hold values from -0.125 to 0.125
- up_weight: bfloat16 [2048, 5632], P('fsdp'), may hold values from -0.125 to 0.125
- down_weight: bfloat16 [5632, 2048], P('fsdp'), may hold values from -0.078125 to 0.078125
Outputs:
- block_out: bfloat16 [8, 1024, 2048], P('fsdp', 'seq')
- input_grad: bfloat16 [8, 1024, 2048], P('fsdp', 'seq')
- first_gain_grad: float32 [2048], P('fsdp')
- first_bias_grad: float32 [2048], P('fsdp')
- qkv_weight_grad: float32 [2048, 6144], P('fsdp')
- qkv_bias_grad: float32 [6144], P('fsdp')
- out_weight_grad: float32 [2048, 2048], P('fsdp')
- second_gain_grad: float32 [2048], P('fsdp')
- second_bias_grad: float32 [2048], P('fsdp')
- gate_weight_grad: float32 [2048, 5632], P('fsdp')
- up_weight_grad: float32 [2048, 5632], P('fsdp')
- down_weight_grad: float32 [5632, 2048], P('fsdp')
Inputs may be any that keep to these rules, and one draw needn't show every extreme that they name: `block_table`: row i holds a pair b and 7 - b, in either order; every block number appears once in the table; the same table holds for all sequences.
All inputs are finite; a program needn't handle non-finite values.
Results may differ from a plain program's by a relative error of at most 0.028.
The roundings to bfloat16 on the way count: a program that leaves them out, or rounds other values in their place, can miss the bound.
Values may be sent and summed in bfloat16 or wider, within the bound.
A program may use at most 448 MiB of HBM per device.

v0:
```python
import functools

import jax
import jax.numpy as jnp
from jax import lax
from jax.experimental import pallas as pl
from jax.experimental.pallas import tpu as pltpu
from jax.sharding import PartitionSpec as P


HD = 64
ROT = HD // 4
HALF = ROT // 2
EPS = 1e-05
ROPE_BASE = 10000.0
NEG = -1e30
SCALE = float(HD) ** -0.5
f32 = jnp.float32
bf16 = jnp.bfloat16


def normalize(values):
    centred = values - jnp.mean(values, axis=-1, keepdims=True)
    inverse = lax.rsqrt(jnp.mean(centred * centred, axis=-1, keepdims=True) + EPS)
    return (centred * inverse, inverse)


def norm_back(d_normed, normed, inverse, gain):
    scaled = d_normed * gain
    return inverse * (
        scaled
        - jnp.mean(scaled, axis=-1, keepdims=True)
        - normed * jnp.mean(scaled * normed, axis=-1, keepdims=True)
    )


def swap(value, mask, n):
    return lax.ppermute(value, "seq", [(i, i ^ mask) for i in range(n)])


def halves(count):
    middle = (count // 2 + 8) // 16 * 16
    return ((0, middle), (middle, count))


def gather_streams(value, n):
    bits = n.bit_length() - 1
    streams = [{0: value[first:last]} for first, last in halves(value.shape[0])]
    for step in range(bits):
        for index, have in enumerate(streams):
            mask = 1 << ((index + step) % bits)
            have.update({key ^ mask: swap(item, mask, n) for key, item in have.items()})
    return [[have[j] for j in range(n)] for have in streams]


def gather_seq(value, n):
    return [jnp.concatenate(pair, axis=0) for pair in zip(*gather_streams(value, n))]


def scatter_seq(pieces, n):
    bits = n.bit_length() - 1
    streams = [
        {j: pieces[j][first:last] for j in range(n)}
        for first, last in halves(pieces[0].shape[0])
    ]
    for step in range(bits):
        for index, have in enumerate(streams):
            mask = 1 << ((index + bits - 1 - step) % bits)
            got = {
                key ^ mask: swap(item.astype(bf16), mask, n)
                for key, item in have.items()
                if key & mask
            }
            streams[index] = {
                key: item + got[key].astype(f32)
                for key, item in have.items()
                if not key & mask
            }
    return jnp.concatenate([have[0] for have in streams], axis=0)


def exchange_seq(pieces, n):
    return [pieces[0]] + [swap(pieces[j], j, n) for j in range(1, n)]


def spread_seq(value, n):
    return exchange_seq([value] * n, n)


def collect_seq(pieces, n):
    got = exchange_seq([pieces[0]] + [piece.astype(bf16) for piece in pieces[1:]], n)
    return sum(item.astype(f32) for item in got)


def choose(index, options):
    out = options[0]
    for i, option in enumerate(options[1:], 1):
        out = jnp.where(index == i, option, out)
    return out


def turn(tensor, cosine, left, right, sign):
    back = pltpu.roll(tensor, 2 * HD - HALF, 1)
    ahead = pltpu.roll(tensor, HALF, 1)
    return tensor * cosine + sign * (back * left + ahead * right)


def attend_kernel(slot_ref, q_ref, k_ref, v_ref, cos_ref, left_ref, right_ref,
                  o_ref, lse_ref, qo_ref, ko_ref, vo_ref, tile):
    tokens = q_ref.shape[0]
    slots = slot_ref.shape[0]
    blk = tokens // slots
    for p in range(slots):
        rows = pl.ds(pl.multiple_of(slot_ref[p] * blk, blk), blk)
        own = pl.ds(p * blk, blk)
        cosine, left, right = cos_ref[own, :], left_ref[own, :], right_ref[own, :]
        qo_ref[own, :] = turn(q_ref[rows, :], cosine, left, right, 1.0).astype(bf16)
        ko_ref[own, :] = turn(k_ref[rows, :], cosine, left, right, 1.0).astype(bf16)
        vo_ref[own, :] = v_ref[rows, :].astype(bf16)
    mask = lax.broadcasted_iota(jnp.int32, (tile, tile), 1) <= lax.broadcasted_iota(
        jnp.int32, (tile, tile), 0
    )
    for t in range(tokens // tile):
        own = pl.ds(t * tile, tile)
        outs, stats = [], []
        for h in range(2):
            lanes = pl.ds(h * HD, HD)
            query = qo_ref[own, lanes]
            end = (t + 1) * tile
            scores = lax.dot_general(
                query, ko_ref[pl.ds(0, end), lanes], (((1,), (1,)), ((), ())),
                preferred_element_type=f32) * SCALE
            diag = jnp.where(mask, scores[:, t * tile :], NEG)
            scores = jnp.concatenate([scores[:, : t * tile], diag], axis=1) if t else diag
            peak = jnp.max(scores, axis=1, keepdims=True)
            weights = jnp.exp(scores - peak)
            total = jnp.sum(weights, axis=1, keepdims=True)
            weights = (weights * (1.0 / total)).astype(bf16)
            outs.append(jnp.dot(weights, vo_ref[pl.ds(0, end), lanes],
                                preferred_element_type=f32))
            stats.append(peak + jnp.log(total))
        out = jnp.concatenate(outs, axis=1).astype(bf16)
        lse_ref[0, own, :] = jnp.concatenate(stats, axis=1)
        for part in range(tile // blk):
            rows = pl.ds(pl.multiple_of(slot_ref[t * (tile // blk) + part] * blk, blk), blk)
            o_ref[rows, :] = out[part * blk : (part + 1) * blk]


def attend(slot, projected, tables, tile=256):
    tokens, width = projected.shape
    width //= 3
    groups = width // (2 * HD)
    lanes = 2 * HD
    col = lambda base: pl.BlockSpec((tokens, lanes), lambda i, s: (0, base + i))
    table = pl.BlockSpec((tokens, lanes), lambda i, s: (0, 0))
    return pl.pallas_call(
        functools.partial(attend_kernel, tile=tile),
        grid_spec=pltpu.PrefetchScalarGridSpec(
            num_scalar_prefetch=1,
            grid=(groups,),
            in_specs=[col(0), col(groups), col(2 * groups), table, table, table],
            out_specs=[col(0), pl.BlockSpec((1, tokens, 2), lambda i, s: (i, 0, 0)),
                       col(0), col(0), col(0)],
        ),
        out_shape=[
            jax.ShapeDtypeStruct((tokens, width), bf16),
            jax.ShapeDtypeStruct((groups, tokens, 2), f32),
            jax.ShapeDtypeStruct((tokens, width), bf16),
            jax.ShapeDtypeStruct((tokens, width), bf16),
            jax.ShapeDtypeStruct((tokens, width), bf16),
        ],
        cost_estimate=pl.CostEstimate(
            flops=4 * tokens * tokens * width, bytes_accessed=24 * tokens * width,
            transcendentals=tokens * tokens * 2 * groups),
        name="attend",
    )(slot, projected, projected, projected, *tables)


def attend_back_kernel(slot_ref, q_ref, k_ref, v_ref, d_ref, lse_ref,
                       cos_ref, left_ref, right_ref, g_ref,
                       d_pos, dq_acc, dk_acc, dv_acc, tile):
    tokens = q_ref.shape[0]
    slots = slot_ref.shape[0]
    blk = tokens // slots
    width = g_ref.shape[1] // 3
    group = pl.program_id(0)
    for p in range(slots):
        rows = pl.ds(pl.multiple_of(slot_ref[p] * blk, blk), blk)
        d_pos[pl.ds(p * blk, blk), :] = d_ref[rows, :]
    dk_acc[...] = jnp.zeros_like(dk_acc)
    dv_acc[...] = jnp.zeros_like(dv_acc)
    mask = lax.broadcasted_iota(jnp.int32, (tile, tile), 0) <= lax.broadcasted_iota(
        jnp.int32, (tile, tile), 1
    )
    for t in range(tokens // tile):
        own = pl.ds(t * tile, tile)
        past = pl.ds(0, (t + 1) * tile)
        grads = []
        keys_grad, values_grad = [], []
        for h in range(2):
            lanes = pl.ds(h * HD, HD)
            query, keys = q_ref[own, lanes], k_ref[past, lanes]
            d_out = d_pos[own, lanes]
            scores = lax.dot_general(keys, query, (((1,), (1,)), ((), ())),
                                     preferred_element_type=f32) * SCALE
            diag = jnp.where(mask, scores[t * tile :], NEG)
            scores = jnp.concatenate([scores[: t * tile], diag], axis=0) if t else diag
            probs = jnp.exp(scores - lse_ref[0, pl.ds(h, 1), own])
            d_probs = lax.dot_general(v_ref[past, lanes], d_out, (((1,), (1,)), ((), ())),
                                      preferred_element_type=f32)
            delta = jnp.sum(d_probs * probs, axis=0, keepdims=True)
            d_scores = (probs * (d_probs - delta)).astype(bf16)
            values_grad.append(jnp.dot(probs.astype(bf16), d_out, preferred_element_type=f32))
            keys_grad.append(jnp.dot(d_scores, query, preferred_element_type=f32))
            grads.append(lax.dot_general(d_scores, keys, (((0,), (0,)), ((), ())),
                                         preferred_element_type=f32))
        dk_acc[past, :] += jnp.concatenate(keys_grad, axis=1)
        dv_acc[past, :] += jnp.concatenate(values_grad, axis=1)
        dq_acc[own, :] = jnp.concatenate(grads, axis=1)
    lanes = 2 * HD
    for p in range(slots):
        rows = pl.ds(pl.multiple_of(slot_ref[p] * blk, blk), blk)
        own = pl.ds(p * blk, blk)
        cosine, left, right = cos_ref[own, :], left_ref[own, :], right_ref[own, :]
        first = pl.multiple_of(group * lanes, lanes)
        g_ref[rows, pl.ds(first, lanes)] = turn(
            dq_acc[own, :] * SCALE, cosine, left, right, -1.0).astype(bf16)
        g_ref[rows, pl.ds(width + first, lanes)] = turn(
            dk_acc[own, :] * SCALE, cosine, left, right, -1.0).astype(bf16)
        g_ref[rows, pl.ds(2 * width + first, lanes)] = dv_acc[own, :].astype(bf16)


def attend_back(slot, query, key, value, d_mixed, lse, tables, tile=256):
    tokens, width = query.shape
    groups = width // (2 * HD)
    lanes = 2 * HD
    col = pl.BlockSpec((tokens, lanes), lambda i, s: (0, i))
    table = pl.BlockSpec((tokens, lanes), lambda i, s: (0, 0))
    return pl.pallas_call(
        functools.partial(attend_back_kernel, tile=tile),
        grid_spec=pltpu.PrefetchScalarGridSpec(
            num_scalar_prefetch=1,
            grid=(groups,),
            in_specs=[col, col, col, col,
                      pl.BlockSpec((1, 2, tokens), lambda i, s: (i, 0, 0)),
                      table, table, table],
            out_specs=pl.BlockSpec((tokens, 3 * width), lambda i, s: (0, 0)),
            scratch_shapes=[pltpu.VMEM((tokens, lanes), bf16)]
            + [pltpu.VMEM((tokens, lanes), f32)] * 3,
        ),
        out_shape=jax.ShapeDtypeStruct((tokens, 3 * width), bf16),
        cost_estimate=pl.CostEstimate(
            flops=10 * tokens * tokens * width, bytes_accessed=16 * tokens * width,
            transcendentals=tokens * tokens * 2 * groups),
        name="attend_back",
    )(slot, query, key, value, d_mixed, lse, *tables)


def finish_kernel(s_ref, *refs, n, steps, outs, place):
    ins, out_refs = refs[:-outs], refs[-outs:]
    for stream in range(len(ins) // n):
        group = ins[stream * n : (stream + 1) * n]

        @pl.when(pl.program_id(0) // steps == stream)
        def _():
            got = [item[...] for item in group]
            place([choose(s_ref[0], [got[i ^ k] for i in range(n)]) for k in range(n)], out_refs)


def finish(s, streams, widths, place, tile):
    n = len(streams[0])
    count, columns = streams[0][0].shape
    steps = count // tile
    rows = count * len(streams)
    specs = []
    for index in range(len(streams)):
        spec = pl.BlockSpec(
            (tile, columns),
            lambda i, s, index=index: (jnp.clip(i - index * steps, 0, steps - 1), 0),
        )
        specs += [spec] * n
    return pl.pallas_call(
        functools.partial(
            finish_kernel, n=n, steps=steps, outs=len(widths), place=place
        ),
        grid_spec=pltpu.PrefetchScalarGridSpec(
            num_scalar_prefetch=1,
            grid=(steps * len(streams),),
            in_specs=specs,
            out_specs=[pl.BlockSpec((tile, width), lambda i, s: (i, 0)) for width in widths],
        ),
        out_shape=[jax.ShapeDtypeStruct((rows, width), f32) for width in widths],
        cost_estimate=pl.CostEstimate(
            flops=0, bytes_accessed=6 * rows * sum(widths), transcendentals=0),
    )(s.reshape(1), *[item for group in streams for item in group])


def place_columns(parts, pieces, outs):
    width = pieces[0].shape[1] // parts
    for c in range(parts):
        for k, item in enumerate(pieces):
            first = (c * len(pieces) + k) * width
            outs[0][:, first : first + width] = item[:, c * width : (c + 1) * width].astype(f32)


def place_units(shards, pieces, outs):
    units = pieces[0].shape[1] // 2
    piece = units // shards
    wide = piece * len(pieces)
    pieces = [item.astype(f32) for item in pieces]
    for base, out in zip((0, units), outs):
        for i in range(shards):
            first = base + i * piece
            out[:, i * wide : (i + 1) * wide] = jnp.concatenate(
                [item[:, first : first + piece] for item in pieces], axis=1
            )


def rope_tables(tokens):
    lane = jnp.arange(2 * HD, dtype=jnp.int32)[None, :] % HD
    turned = lane < ROT
    freq = ROPE_BASE ** (-((lane % HALF).astype(f32) * 2.0) / ROT)
    angle = jnp.arange(tokens, dtype=jnp.int32)[:, None].astype(f32) * freq
    sine = jnp.sin(angle)
    return (
        jnp.where(turned, jnp.cos(angle), 1.0),
        jnp.where(lane < HALF, -sine, 0.0),
        jnp.where(turned & (lane >= HALF), sine, 0.0),
    )


def body(
    hidden_in,
    cotangent,
    block_table,
    first_gain,
    first_bias,
    qkv_weight,
    qkv_bias,
    out_weight,
    second_gain,
    second_bias,
    gate_weight,
    up_weight,
    down_weight,
    *,
    n,
    fs,
):
    s = lax.axis_index("seq")
    inputs = hidden_in[0].astype(f32)
    own, width = inputs.shape
    part = width // n
    rows = width // fs
    ffn = gate_weight.shape[1]
    units = ffn // n
    shard = ffn // fs
    piece = units // fs
    tokens = n * own
    order = [s ^ j for j in range(n)]

    blocks = jnp.concatenate(
        [lax.dynamic_slice_in_dim(block_table, order[j], 1, 0)[0] for j in range(n)]
    )
    ids = jnp.arange(2 * n, dtype=jnp.int32)
    slot = jnp.sum(jnp.where(blocks[None, :] == ids[:, None], ids[None, :], 0), axis=1)
    tables = rope_tables(tokens)

    def gather_fsdp(value):
        return lax.all_gather(value, "fsdp", axis=0, tiled=True)

    after = lambda value, first: lax.optimization_barrier((value, first))[0]

    small = jnp.concatenate([first_gain, first_bias, second_gain, second_bias, qkv_bias])
    small = lax.all_gather(small, "fsdp", axis=0)
    vec = lambda i: small[:, i * rows : (i + 1) * rows].reshape(width).astype(f32)
    gain_one, bias_one, gain_two, bias_two = (vec(i) for i in range(4))
    bias_qkv = small[:, 4 * rows :].reshape(3, width).astype(f32)

    qkv_part = choose(
        s,
        [
            jnp.concatenate(
                [
                    qkv_weight[:, c * width + i * part : c * width + (i + 1) * part]
                    for c in range(3)
                ],
                axis=1,
            )
            for i in range(n)
        ],
    )
    out_part = choose(s, [out_weight[:, i * part : (i + 1) * part] for i in range(n)])
    w_first = gather_fsdp(jnp.concatenate([qkv_part, out_part], axis=1))
    w_qkv = w_first[:, : 3 * part]

    normed_one, inverse_one = normalize(inputs)
    h1_own = (normed_one * gain_one + bias_one).astype(bf16)
    picked = jnp.arange(units, dtype=jnp.int32)
    picked = (picked // piece) * shard + s * piece + picked % piece
    picked = after(picked, h1_own)
    pick = (jnp.arange(ffn, dtype=jnp.int32)[:, None] == picked[None, :]).astype(bf16)
    gate_up = jnp.concatenate(
        [
            jnp.dot(gate_weight, pick, preferred_element_type=f32).astype(bf16),
            jnp.dot(up_weight, pick, preferred_element_type=f32).astype(bf16),
        ],
        axis=1,
    )
    w_gate_up = gather_fsdp(gate_up)
    w_down = gather_fsdp(choose(s, [down_weight[i * piece : (i + 1) * piece] for i in range(n)]))

    h1 = jnp.concatenate(gather_seq(h1_own, n), axis=0)
    core = lax.axis_index("fsdp") % 2
    half = width // 2
    w_out_half = choose(core, [w_first[:half, 3 * part :], w_first[half:, 3 * part :]])
    w_out_pieces = gather_seq(after(w_out_half, h1), n)
    bias_part = choose(s, [bias_qkv[:, i * part : (i + 1) * part] for i in range(n)])
    projected = jnp.dot(h1, w_qkv, preferred_element_type=f32)
    projected = projected + bias_part.reshape(3 * part)
    head_out, lse, query, key, value = attend(slot, projected, tables)

    def natural(pieces):
        return [choose(s, [pieces[i ^ k] for i in range(n)]) for k in range(n)]

    def to_columns(pieces):
        return jnp.concatenate(natural(pieces), axis=1)

    def column_parts(value):
        return natural([value[:, k * part : (k + 1) * part] for k in range(n)])

    mixed = to_columns(
        exchange_seq([head_out[j * own : (j + 1) * own] for j in range(n)], n)
    )
    w_out = to_columns(w_out_pieces)
    w_out = [w_out, lax.ppermute(w_out, "fsdp", [(i, i ^ 1) for i in range(fs)])]
    by_core = lambda a, b: [jnp.where(core == 0, a, b), jnp.where(core == 0, b, a)]
    mixed_first, mixed_second = by_core(mixed[:, :half], mixed[:, half:])
    residual = (
        inputs
        + jnp.dot(mixed_first, w_out[0], preferred_element_type=f32)
        + jnp.dot(mixed_second, w_out[1], preferred_element_type=f32)
    )

    normed_two, inverse_two = normalize(residual)
    h2 = jnp.concatenate(gather_seq((normed_two * gain_two + bias_two).astype(bf16), n), axis=0)
    d_own = cotangent[0]
    d_branch = jnp.concatenate(gather_seq(after(d_own, h2), n), axis=0)
    gate = jnp.dot(h2, w_gate_up, preferred_element_type=f32)
    gate, upward = gate[:, :units], gate[:, units:]
    sigmoid = jax.nn.sigmoid(gate)
    activated = (gate * sigmoid * upward).astype(bf16)
    across = (((1,), (1,)), ((), ()))
    down = (((0,), (0,)), ((), ()))
    dot = functools.partial(lax.dot_general, preferred_element_type=f32)

    def scatter_fsdp(value):
        return lax.psum_scatter(value, "fsdp", scatter_dimension=0, tiled=True)

    down_term = dot(activated, d_branch, down).astype(bf16)
    down_grad = scatter_fsdp(down_term)
    mixed_all = jnp.concatenate(gather_seq(after(mixed, d_branch), n), axis=0)
    branch = dot(after(activated, down_term), w_down, (((1,), (0,)), ((), ())))
    d_activated = dot(after(d_branch, branch), w_down, across)
    branch = collect_seq([branch[j * own : (j + 1) * own] for j in range(n)], n)
    block_out = (residual + branch).astype(bf16)
    d_gate_up = jnp.concatenate(
        [
            (d_activated * upward * sigmoid * (1.0 + gate * (1.0 - sigmoid))).astype(bf16),
            (d_activated * gate * sigmoid).astype(bf16),
        ],
        axis=1,
    )
    gate_up_term = dot(h2, d_gate_up, down).astype(bf16)
    gate_up_grad = scatter_fsdp(gate_up_term)
    d_h2 = dot(after(d_gate_up, gate_up_term), w_gate_up, across)
    d_h2 = scatter_seq([d_h2[j * own : (j + 1) * own] for j in range(n)], n)
    gain_two_grad = jnp.sum(d_h2 * normed_two, axis=0)
    bias_two_grad = jnp.sum(d_h2, axis=0)
    d_residual = d_own.astype(f32) + norm_back(d_h2, normed_two, inverse_two, gain_two)

    d_attended = d_residual.astype(bf16)
    d_mixed = by_core(*[dot(d_attended, item, across).astype(bf16) for item in w_out])
    d_mixed = jnp.concatenate(d_mixed, axis=1)
    d_mixed = jnp.concatenate(exchange_seq(column_parts(d_mixed), n), axis=0)
    d_projected = attend_back(
        slot, query, key, value, d_mixed, lse.transpose(0, 2, 1), tables
    )
    d_attended_part = exchange_seq(column_parts(after(d_attended, d_mixed)), n)
    d_attended_part = jnp.concatenate(d_attended_part, axis=0)
    down_pieces = spread_seq(after(down_grad, d_mixed), n)
    out_term = dot(mixed_all, d_attended_part, down).astype(bf16)
    qkv_term = dot(h1, d_projected, down).astype(bf16)
    qkv_grad = scatter_fsdp(qkv_term)
    qkv_bias_part = jnp.sum(d_projected.astype(f32), axis=0)
    d_h1 = dot(after(d_projected, qkv_term), w_qkv, across)
    d_h1 = scatter_seq([d_h1[j * own : (j + 1) * own] for j in range(n)], n)
    gain_one_grad = jnp.sum(d_h1 * normed_one, axis=0)
    bias_one_grad = jnp.sum(d_h1, axis=0)
    input_grad = (
        d_residual + norm_back(d_h1, normed_one, inverse_one, gain_one)
    ).astype(bf16)

    bias_all = jnp.concatenate(
        [jnp.where(s == i, qkv_bias_part.reshape(3, part), 0.0) for i in range(n)], axis=1
    )
    small = [
        gain_one_grad.reshape(fs, rows),
        bias_one_grad.reshape(fs, rows),
        gain_two_grad.reshape(fs, rows),
        bias_two_grad.reshape(fs, rows),
        bias_all.reshape(fs, 3 * rows),
    ]
    extra = -(-7 * rows // part)
    extra += -extra % 16
    small.append(jnp.zeros((fs, extra * part - 7 * rows), f32))
    small = jnp.concatenate(small, axis=1).astype(bf16).reshape(fs, extra, part)
    out_term = jnp.concatenate([out_term.reshape(fs, rows, part), small], axis=1)
    out_grad = scatter_fsdp(out_term.reshape(fs * (rows + extra), part))

    down_total = jnp.stack(natural(down_pieces)).reshape(shard, width).astype(f32)
    gate_up_pieces = gather_streams(after(gate_up_grad, d_h1), n)
    gate_total, up_total = finish(
        s, gate_up_pieces, (ffn, ffn),
        functools.partial(place_units, fs), min(64, rows // 2))
    qkv_pieces = gather_streams(after(qkv_grad, gate_up_pieces[0][n - 1]), n)
    (qkv_total,) = finish(
        s, qkv_pieces, (3 * width,),
        functools.partial(place_columns, 3), min(64, rows // 2))
    out_pieces = spread_seq(out_grad, n)
    (out_total,) = finish(
        s, [[got[:rows] for got in out_pieces]], (width,),
        functools.partial(place_columns, 1), rows)
    sums = sum(got[rows:].astype(f32) for got in out_pieces).reshape(extra * part)
    return (
        block_out[None],
        input_grad[None],
        sums[:rows],
        sums[rows : 2 * rows],
        qkv_total,
        sums[4 * rows : 7 * rows],
        out_total,
        sums[2 * rows : 3 * rows],
        sums[3 * rows : 4 * rows],
        gate_total,
        up_total,
        down_total,
    )


def solution(mesh):
    split = P("fsdp", None)
    act = P("fsdp", "seq", None)
    vec = P("fsdp")
    return jax.shard_map(
        functools.partial(body, n=mesh.shape["seq"], fs=mesh.shape["fsdp"]),
        mesh=mesh,
        in_specs=(act, act, P(), vec, vec, split, vec, split, vec, vec, split, split, split),
        out_specs=(act, act, vec, vec, split, vec, split, vec, vec, split, split, split),
        check_vma=False,
    )
```

profile of v0, /device:TPU:0, one launch (start us, length us, event | category | flops | bytes accessed | tf_op | source)
XLA Modules:
  0.0 831.7 jit_solution(16469066590874045435)
XLA Ops:
  12.2 15.8 %all-gather.1 = bf16[8,1,1792]{2,1,0:T(2,128)(2,1)S(1)} all-gather(bf16[1,1,1792]{2,1,0:T(2,128)(2,1)S(1)} %reshape.237), channel_id=2, replica_groups=mesh['seq'=4,'fsdp'=8] {'fsdp'}, dimensions={0}, use_global_device_ids=true | all-gather | bytes 32256 | tf_op jit(solution)/shard_map/all_gather | solution.py:375
  49.9 11.0 %collective-permute-done.3 = bf16[128,2048]{1,0:T(8,128)(2,1)S(1)} collective-permute-done((bf16[128,2048]{1,0:T(8,128)(2,1)}, bf16[128,2048]{1,0:T(8,128)(2,1)S(1)}, u32[]{:S(2)}, u32[]{:S(2)}) %collective-permute-start.3) | collective-permute-done | bytes 524320 | tf_op jit(solution)/shard_map/ppermute | solution.py:38
  84.6 11.5 %all-gather.6.cloned.1.call-done = bf16[2048,2048]{1,0:T(8,128)(2,1)} async-done(((bf16[256,2048]{1,0:T(8,128)(2,1)}), bf16[2048,2048]{1,0:T(8,128)(2,1)}) %all-gather.6.cloned.1.call-update) | async-done | bytes 8388624 | tf_op jit(solution)/shard_map/all_gather | solution.py:370
  102.9 11.0 %collective-permute-done.9 = bf16[512,512]{1,0:T(8,128)(2,1)S(1)} collective-permute-done((bf16[512,512]{1,0:T(8,128)(2,1)}, bf16[512,512]{1,0:T(8,128)(2,1)S(1)}, u32[]{:S(2)}, u32[]{:S(2)}) %collective-permute-start.9) | collective-permute-done | bytes 524320 | tf_op jit(solution)/shard_map/ppermute | solution.py:38
  117.0 9.7 %collective-permute-done.13 = bf16[512,512]{1,0:T(8,128)(2,1)} collective-permute-done((bf16[512,512]{1,0:T(8,128)(2,1)}, bf16[512,512]{1,0:T(8,128)(2,1)}, u32[]{:S(2)}, u32[]{:S(2)}) %collective-permute-start.13) | collective-permute-done | bytes 524320 | tf_op jit(solution)/shard_map/ppermute | solution.py:38
  144.4 11.7 %fusion.11.q_ref.k_ref.v_ref = f32[1024,1536]{1,0:T(8,128)} fusion(bf16[1024,2048]{1,0:T(8,128)(2,1)} %constant_dynamic-update-slice_fusion, bf16[2048,2048]{1,0:T(8,128)(2,1)} %all-gather.6.cloned.1.call-done, f32[1536]{0:T(1024)S(1)} %add.214), kind=kOutput, calls=%fused_computation.19 | convolution fusion | flops 6444023808 | bytes 16783360 | tf_op jit(solution)/shard_map/dot_general | solution.py:419
  156.1 23.9 %attend.1 = (bf16[1024,512]{1,0:T(8,128)(2,1)}, f32[4,1024,2]{2,1,0:T(8,128)}, bf16[1024,512]{1,0:T(8,128)(2,1)}, bf16[1024,512]{1,0:T(8,128)(2,1)}, bf16[1024,512]{1,0:T(8,128)(2,1)}) custom-call(s32[8]{0:T(128)} %select_reduce_fusion.slot_ref, f32[1024,1536]{1,0:T(8,128)} %fusion.11.q_ref.k_ref.v_ref, f32[1024,1536]{1,0:T(8,128)} %fusion.11.q_ref.k_ref.v_ref, ...), custom_call_target="tpu_custom_call" | custom-call | flops 2147483648 | bytes 12582912 | tf_op jit(solution)/shard_map/attend/pallas_call | solution.py:156
  213.1 9.8 %collective-permute-done.19 = bf16[128,2048]{1,0:T(8,128)(2,1)} collective-permute-done((bf16[128,2048]{1,0:T(8,128)(2,1)}, bf16[128,2048]{1,0:T(8,128)(2,1)}, u32[]{:S(2)}, u32[]{:S(2)}) %collective-permute-start.19) | collective-permute-done | bytes 524320 | tf_op jit(solution)/shard_map/ppermute | solution.py:38
  252.8 17.4 %fusion.122 = f32[1024,2816]{1,0:T(8,128)S(1)} fusion(bf16[1024,2048]{1,0:T(8,128)(2,1)} %constant_dynamic-update-slice_fusion.13, bf16[2048,2816]{0,1:T(8,128)(2,1)} %all-gather.8.cloned.1.call-done), kind=kOutput, calls=%fused_computation.263 | convolution fusion | flops 11811160064 | bytes 27262976 | tf_op jit(solution)/shard_map/dot_general | solution.py:449
  297.1 12.4 %fusion.120 = (bf16[1024,2048]{1,0:T(8,128)(2,1)}, f32[1024,2048]{1,0:T(8,128)}) fusion(bf16[1024,1408]{1,0:T(8,128)(2,1)} %copy-done.10, bf16[1408,2048]{1,0:T(8,128)(2,1)} %all-gather.10.cloned.1.call-done), kind=kOutput, calls=%fused_computation.261 | convolution fusion | flops 5907677184 | bytes 21233664 | tf_op jit(solution)/shard_map/dot_general | solution.py:463
  309.6 12.6 %multiply_convert_fusion.1 = (bf16[1024,1408]{1,0:T(8,128)(2,1)S(1)}, bf16[1024,1408]{1,0:T(8,128)(2,1)S(1)}) fusion(f32[1024,2816]{1,0:T(8,128)} %copy-done.4, bf16[1024,2048]{1,0:T(8,128)(2,1)S(1)} %copy-done.24, bf16[1408,2048]{1,0:T(8,128)(2,1)} %all-gather.10.cloned.1.call-done), kind=kOutput, calls=%fused_computation.12 | convolution fusion | flops 5924323328 | bytes 27262976 | tf_op jit(solution)/shard_map/dot_general | solution.py:464
  324.6 18.2 %convolution_convert_fusion = bf16[2048,2816]{1,0:T(8,128)(2,1)} fusion(bf16[1024,2048]{1,0:T(8,128)(2,1)} %constant_dynamic-update-slice_fusion.13, bf16[1024,1408]{1,0:T(8,128)(2,1)S(1)} %get-tuple-element.75, bf16[1024,1408]{1,0:T(8,128)(2,1)S(1)} %get-tuple-element.74), kind=kOutput, calls=%fused_computation.6 | convolution fusion | flops 11828461568 | bytes 21495808 | tf_op jit(solution)/shard_map/dot_general | solution.py:474
  349.9 17.4 %fusion.119 = (bf16[1024,2048]{1,0:T(8,128)(2,1)S(1)}, f32[1024,2048]{1,0:T(8,128)}) fusion(bf16[1024,2816]{1,0:T(8,128)(2,1)S(1)} %pad_maximum_fusion, bf16[2048,2816]{0,1:T(8,128)(2,1)} %all-gather.8.cloned.1.call-done), kind=kOutput, calls=%fused_computation.260 | convolution fusion | flops 11813257216 | bytes 29884416 | tf_op jit(solution)/shard_map/dot_general | solution.py:476
  385.2 15.5 %collective-permute-done.31 = bf16[128,2048]{1,0:T(8,128)(2,1)S(1)} collective-permute-done((bf16[128,2048]{1,0:T(8,128)(2,1)S(1)}, bf16[128,2048]{1,0:T(8,128)(2,1)S(1)}, u32[]{:S(2)}, u32[]{:S(2)}) %collective-permute-start.31) | collective-permute-done | bytes 524320 | tf_op jit(solution)/shard_map/ppermute | solution.py:38
  432.6 17.9 %collective-permute-done.28 = bf16[256,2048]{1,0:T(8,128)(2,1)S(1)} collective-permute-done((bf16[256,2048]{1,0:T(8,128)(2,1)S(1)}, bf16[256,2048]{1,0:T(8,128)(2,1)S(1)}, u32[]{:S(2)}, u32[]{:S(2)}) %collective-permute-start.28) | collective-permute-done | bytes 1048608 | tf_op jit(solution)/shard_map/ppermute | solution.py:38
  450.5 23.1 %collective-permute-done.30 = bf16[256,2048]{1,0:T(8,128)(2,1)S(1)} collective-permute-done((bf16[256,2048]{1,0:T(8,128)(2,1)S(1)}, bf16[256,2048]{1,0:T(8,128)(2,1)S(1)}, u32[]{:S(2)}, u32[]{:S(2)}) %collective-permute-start.30) | collective-permute-done | bytes 1048608 | tf_op jit(solution)/shard_map/ppermute | solution.py:38
  496.9 26.4 %attend_back.1 = bf16[1024,1536]{1,0:T(8,128)(2,1)} custom-call(s32[8]{0:T(128)} %select_reduce_fusion.slot_ref, bf16[1024,512]{1,0:T(8,128)(2,1)} %get-tuple-element.38.q_ref, bf16[1024,512]{1,0:T(8,128)(2,1)} %get-tuple-element.39.k_ref, bf16[1024,512]{1,0:T(8,128)(2,1)} %get-tuple-element.40.v_ref, bf16[1024,512]{1,0:T(8,128)(2,1)} %pad_maximum_fusion.8.d_ref, ...), custom_call_target="tpu_custom_call" | custom-call | flops 5368709120 | bytes 8388608 | tf_op jit(solution)/shard_map/attend_back/pallas_call | solution.py:239
  523.3 11.4 %convolution_convert_fusion.1 = bf16[2048,1536]{1,0:T(8,128)(2,1)} fusion(bf16[1024,2048]{1,0:T(8,128)(2,1)} %constant_dynamic-update-slice_fusion, bf16[1024,1536]{1,0:T(8,128)(2,1)} %attend_back.1), kind=kOutput, calls=%fused_computation.7 | convolution fusion | flops 6445596672 | bytes 13631488 | tf_op jit(solution)/shard_map/dot_general | solution.py:493
  534.7 12.0 %fusion.121 = (bf16[1024,2048]{1,0:T(8,128)(2,1)S(1)}, f32[1024,2048]{1,0:T(8,128)}) fusion(bf16[1024,1536]{1,0:T(8,128)(2,1)} %attend_back.1, bf16[2048,2048]{1,0:T(8,128)(2,1)} %all-gather.6.cloned.1.call-done), kind=kOutput, calls=%fused_computation.262 | convolution fusion | flops 6444548096 | bytes 22020096 | tf_op jit(solution)/shard_map/dot_general | solution.py:496
  606.8 28.6 %reduce-scatter.5.cloned.1.call-done = bf16[272,512]{1,0:T(8,128)(2,1)} async-done(((bf16[2176,512]{1,0:T(8,128)(2,1)}), bf16[272,512]{1,0:T(8,128)(2,1)}) %reduce-scatter.5.cloned.1.call-update) | async-done | bytes 278544 | tf_op jit(solution)/shard_map/reduce_scatter | solution.py:458
  644.7 57.0 %reduce-scatter.11.cloned.1.call-done = bf16[176,2048]{1,0:T(8,128)(2,1)} async-done(((bf16[1408,2048]{1,0:T(8,128)(2,1)}), bf16[176,2048]{1,0:T(8,128)(2,1)}) %reduce-scatter.11.cloned.1.call-update) | async-done | bytes 720912 | tf_op jit(solution)/shard_map/reduce_scatter | solution.py:458
  716.9 55.8 %reduce-scatter.7.cloned.1.call-done = bf16[256,1536]{1,0:T(8,128)(2,1)} async-done(((bf16[2048,1536]{1,0:T(8,128)(2,1)}), bf16[256,1536]{1,0:T(8,128)(2,1)}) %reduce-scatter.7.cloned.1.call-update) | async-done | bytes 786448 | tf_op jit(solution)/shard_map/reduce_scatter | solution.py:458
  782.7 11.2 %collective-permute-done.66.refs_2_ = bf16[128,2816]{1,0:T(8,128)(2,1)S(1)} collective-permute-done((bf16[128,2816]{1,0:T(8,128)(2,1)}, bf16[128,2816]{1,0:T(8,128)(2,1)S(1)}, u32[]{:S(2)}, u32[]{:S(2)}) %collective-permute-start.66) | collective-permute-done | bytes 720928 | tf_op jit(solution)/shard_map/ppermute | solution.py:38
  808.9 9.7 %shard_map.222 = (f32[256,5632]{1,0:T(8,128)}, f32[256,5632]{1,0:T(8,128)}) custom-call(s32[1]{0:T(128)} %bitcast.9.s_ref, bf16[128,2816]{1,0:T(8,128)(2,1)} %get-tuple-element.115.refs_0_, bf16[128,2816]{1,0:T(8,128)(2,1)} %copy-done.17, bf16[128,2816]{1,0:T(8,128)(2,1)} %copy-done.19, bf16[128,2816]{1,0:T(8,128)(2,1)} %collective-permute-done.59.refs_3_, ...), custom_call_target="tpu_custom_call" | custom-call | bytes 17301504 | tf_op jit(solution)/shard_map/pallas_call | solution.py:282
  (383 shorter events, 365.0 us)
Async XLA Ops:
  7.2 89.0 %all-gather.6.cloned.1.call-start = ((), (), s32[]{:S(2)}) async-start(), calls=%async_computation.4 | async-start | bytes 9437184 | tf_op jit(solution)/shard_map/all_gather | solution.py:370
  11.2 241.6 %all-gather.8.cloned.1.call-start = ((), (), s32[]{:S(2)}) async-start(), calls=%async_computation.5 | async-start | bytes 12976128 | tf_op jit(solution)/shard_map/all_gather | solution.py:370
  44.4 252.7 %all-gather.10.cloned.1.call-start = ((), (), s32[]{:S(2)}) async-start(), calls=%async_computation.6 | async-start | bytes 6488064 | tf_op jit(solution)/shard_map/all_gather | solution.py:370
  140.2 57.6 %collective-permute-start.15 = (bf16[1024,2048]{1,0:T(8,128)(2,1)}, bf16[1024,2048]{1,0:T(8,128)(2,1)}, u32[]{:S(2)}, u32[]{:S(2)}) collective-permute-start(bf16[1024,2048]{1,0:T(8,128)(2,1)} %pad_maximum_fusion.1), channel_id=1, source_target_pairs={{0,1},{1,0},{2,3},{3,2},{4,5},{5,4},{6,7},{7,6},{8,9},{9,8},{10,11... | collective-permute-start | bytes 12582920 | tf_op jit(solution)/shard_map/ppermute | solution.py:436
  212.9 390.4 %reduce-scatter.9.cloned.1.call-start = ((), (), s32[]{:S(2)}) async-start(), calls=%async_computation.9 | async-start | bytes 12976128 | tf_op jit(solution)/shard_map/reduce_scatter | solution.py:458
  342.9 292.5 %reduce-scatter.5.cloned.1.call-start = ((), (), s32[]{:S(2)}) async-start(), calls=%async_computation.7 | async-start | bytes 2506752 | tf_op jit(solution)/shard_map/reduce_scatter | solution.py:458
  369.0 50.6 %collective-permute-start.49 = (bf16[128,2048]{1,0:T(8,128)(2,1)S(1)}, bf16[128,2048]{1,0:T(8,128)(2,1)S(1)}, u32[]{:S(2)}, u32[]{:S(2)}) collective-permute-start(bf16[128,2048]{1,0:T(8,128)(2,1)S(1)} %get-tuple-element.120), channel_id=1, source_target_pairs={{0,16},{8,24},{16,0},{24,8},{1,17},{9,25},{17,1},{25,9},{2,18},{10... | collective-permute-start | bytes 1572872 | tf_op jit(solution)/shard_map/ppermute | solution.py:38
  369.8 38.7 %collective-permute-start.46 = (bf16[128,2048]{1,0:T(8,128)(2,1)S(1)}, bf16[128,2048]{1,0:T(8,128)(2,1)S(1)}, u32[]{:S(2)}, u32[]{:S(2)}) collective-permute-start(bf16[128,2048]{1,0:T(8,128)(2,1)S(1)} %get-tuple-element.121), channel_id=1, source_target_pairs={{0,8},{8,0},{16,24},{24,16},{1,9},{9,1},{17,25},{25,17},{2,10},{10... | collective-permute-start | bytes 1572872 | tf_op jit(solution)/shard_map/ppermute | solution.py:38
  417.9 55.7 %collective-permute-start.30 = (bf16[256,2048]{1,0:T(8,128)(2,1)S(1)}, bf16[256,2048]{1,0:T(8,128)(2,1)S(1)}, u32[]{:S(2)}, u32[]{:S(2)}) collective-permute-start(bf16[256,2048]{1,0:T(8,128)(2,1)S(1)} %get-tuple-element.87), channel_id=1, source_target_pairs={{0,24},{8,16},{16,8},{24,0},{1,25},{9,17},{17,9},{25,1},{2,26},{10... | collective-permute-start | bytes 3145736 | tf_op jit(solution)/shard_map/ppermute | solution.py:38
  419.6 54.0 %collective-permute-start.29 = (bf16[256,2048]{1,0:T(8,128)(2,1)S(1)}, bf16[256,2048]{1,0:T(8,128)(2,1)S(1)}, u32[]{:S(2)}, u32[]{:S(2)}) collective-permute-start(bf16[256,2048]{1,0:T(8,128)(2,1)S(1)} %get-tuple-element.88), channel_id=1, source_target_pairs={{0,16},{8,24},{16,0},{24,8},{1,17},{9,25},{17,1},{25,9},{2,18},{10... | collective-permute-start | bytes 3145736 | tf_op jit(solution)/shard_map/ppermute | solution.py:38
  428.0 61.2 %collective-permute-start.50 = (bf16[128,2048]{1,0:T(8,128)(2,1)S(1)}, bf16[128,2048]{1,0:T(8,128)(2,1)S(1)}, u32[]{:S(2)}, u32[]{:S(2)}) collective-permute-start(bf16[128,2048]{1,0:T(8,128)(2,1)S(1)} %collective-permute-done.46), channel_id=1, source_target_pairs={{0,16},{8,24},{16,0},{24,8},{1,17},{9,25},{17,1},{25,9},{2,18},{10... | collective-permute-start | bytes 1572872 | tf_op jit(solution)/shard_map/ppermute | solution.py:38
  429.2 119.8 %collective-permute-start.51 = (bf16[128,2048]{1,0:T(8,128)(2,1)S(1)}, bf16[128,2048]{1,0:T(8,128)(2,1)S(1)}, u32[]{:S(2)}, u32[]{:S(2)}) collective-permute-start(bf16[128,2048]{1,0:T(8,128)(2,1)S(1)} %collective-permute-done.49), channel_id=1, source_target_pairs={{0,8},{8,0},{16,24},{24,16},{1,9},{9,1},{17,25},{25,17},{2,10},{10... | collective-permute-start | bytes 1572872 | tf_op jit(solution)/shard_map/ppermute | solution.py:38
  602.0 99.6 %reduce-scatter.11.cloned.1.call-start = ((), (), s32[]{:S(2)}) async-start(), calls=%async_computation.10 | async-start | bytes 6488064 | tf_op jit(solution)/shard_map/reduce_scatter | solution.py:458
  602.6 170.2 %reduce-scatter.7.cloned.1.call-start = ((), (), s32[]{:S(2)}) async-start(), calls=%async_computation.8 | async-start | bytes 7077888 | tf_op jit(solution)/shard_map/reduce_scatter | solution.py:458
  635.3 67.8 %collective-permute-start.57 = (bf16[272,512]{1,0:T(8,128)(2,1)}, bf16[272,512]{1,0:T(8,128)(2,1)S(1)}, u32[]{:S(2)}, u32[]{:S(2)}) collective-permute-start(bf16[272,512]{1,0:T(8,128)(2,1)} %reduce-scatter.5.cloned.1.call-done), channel_id=1, source_target_pairs={{0,24},{8,16},{16,8},{24,0},{1,25},{9,17},{17,9},{25,1},{2,26},{10... | collective-permute-start | bytes 835592 | tf_op jit(solution)/shard_map/ppermute | solution.py:38
  637.7 66.9 %collective-permute-start.56 = (bf16[272,512]{1,0:T(8,128)(2,1)}, bf16[272,512]{1,0:T(8,128)(2,1)}, u32[]{:S(2)}, u32[]{:S(2)}) collective-permute-start(bf16[272,512]{1,0:T(8,128)(2,1)} %reduce-scatter.5.cloned.1.call-done), channel_id=1, source_target_pairs={{0,16},{8,24},{16,0},{24,8},{1,17},{9,25},{17,1},{25,9},{2,18},{10... | collective-permute-start | bytes 835592 | tf_op jit(solution)/shard_map/ppermute | solution.py:38
  638.3 66.9 %collective-permute-start.55 = (bf16[272,512]{1,0:T(8,128)(2,1)}, bf16[272,512]{1,0:T(8,128)(2,1)}, u32[]{:S(2)}, u32[]{:S(2)}) collective-permute-start(bf16[272,512]{1,0:T(8,128)(2,1)} %reduce-scatter.5.cloned.1.call-done), channel_id=1, source_target_pairs={{0,8},{8,0},{16,24},{24,16},{1,9},{9,1},{17,25},{25,17},{2,10},{10... | collective-permute-start | bytes 835592 | tf_op jit(solution)/shard_map/ppermute | solution.py:38
  638.8 76.6 %collective-permute-start.59 = (bf16[128,2816]{1,0:T(8,128)(2,1)S(1)}, bf16[128,2816]{1,0:T(8,128)(2,1)}, u32[]{:S(2)}, u32[]{:S(2)}) collective-permute-start(bf16[128,2816]{1,0:T(8,128)(2,1)S(1)} %collective-permute-done.58.refs_1_), channel_id=1, source_target_pairs={{0,16},{8,24},{16,0},{24,8},{1,17},{9,25},{17,1},{25,9},{2,18},{10... | collective-permute-start | bytes 2162696 | tf_op jit(solution)/shard_map/ppermute | solution.py:38
  701.7 73.0 %collective-permute-start.72 = (bf16[176,2048]{1,0:T(8,128)(2,1)}, bf16[176,2048]{1,0:T(8,128)(2,1)S(1)}, u32[]{:S(2)}, u32[]{:S(2)}) collective-permute-start(bf16[176,2048]{1,0:T(8,128)(2,1)} %reduce-scatter.11.cloned.1.call-done), channel_id=1, source_target_pairs={{0,8},{8,0},{16,24},{24,16},{1,9},{9,1},{17,25},{25,17},{2,10},{10... | collective-permute-start | bytes 2162696 | tf_op jit(solution)/shard_map/ppermute | solution.py:38
  703.1 73.0 %collective-permute-start.71 = (bf16[176,2048]{1,0:T(8,128)(2,1)}, bf16[176,2048]{1,0:T(8,128)(2,1)}, u32[]{:S(2)}, u32[]{:S(2)}) collective-permute-start(bf16[176,2048]{1,0:T(8,128)(2,1)} %reduce-scatter.11.cloned.1.call-done), channel_id=1, source_target_pairs={{0,16},{8,24},{16,0},{24,8},{1,17},{9,25},{17,1},{25,9},{2,18},{10... | collective-permute-start | bytes 2162696 | tf_op jit(solution)/shard_map/ppermute | solution.py:38
  704.6 72.1 %collective-permute-start.70 = (bf16[176,2048]{1,0:T(8,128)(2,1)}, bf16[176,2048]{1,0:T(8,128)(2,1)}, u32[]{:S(2)}, u32[]{:S(2)}) collective-permute-start(bf16[176,2048]{1,0:T(8,128)(2,1)} %reduce-scatter.11.cloned.1.call-done), channel_id=1, source_target_pairs={{0,24},{8,16},{16,8},{24,0},{1,25},{9,17},{17,9},{25,1},{2,26},{10... | collective-permute-start | bytes 2162696 | tf_op jit(solution)/shard_map/ppermute | solution.py:38
  714.0 65.9 %collective-permute-start.68 = (bf16[128,2816]{1,0:T(8,128)(2,1)}, bf16[128,2816]{1,0:T(8,128)(2,1)}, u32[]{:S(2)}, u32[]{:S(2)}) collective-permute-start(bf16[128,2816]{1,0:T(8,128)(2,1)} %get-tuple-element.114.refs_4_), channel_id=1, source_target_pairs={{0,16},{8,24},{16,0},{24,8},{1,17},{9,25},{17,1},{25,9},{2,18},{10... | collective-permute-start | bytes 2162696 | tf_op jit(solution)/shard_map/ppermute | solution.py:38
  715.5 65.7 %collective-permute-start.67 = (bf16[128,2816]{1,0:T(8,128)(2,1)}, bf16[128,2816]{1,0:T(8,128)(2,1)}, u32[]{:S(2)}, u32[]{:S(2)}) collective-permute-start(bf16[128,2816]{1,0:T(8,128)(2,1)} %get-tuple-element.114.refs_4_), channel_id=1, source_target_pairs={{0,8},{8,0},{16,24},{24,16},{1,9},{9,1},{17,25},{25,17},{2,10},{10... | collective-permute-start | bytes 2162696 | tf_op jit(solution)/shard_map/ppermute | solution.py:38
  781.1 37.5 %collective-permute-start.63 = (bf16[128,1536]{1,0:T(8,128)(2,1)S(1)}, bf16[128,1536]{1,0:T(8,128)(2,1)}, u32[]{:S(2)}, u32[]{:S(2)}) collective-permute-start(bf16[128,1536]{1,0:T(8,128)(2,1)S(1)} %get-tuple-element.139.refs_4_), channel_id=1, source_target_pairs={{0,8},{8,0},{16,24},{24,16},{1,9},{9,1},{17,25},{25,17},{2,10},{10... | collective-permute-start | bytes 1179656 | tf_op jit(solution)/shard_map/ppermute | solution.py:38
  (94 other events, 1580.2 us)
Sparse Core Ops, SparseCore 0:
  11.3 84.8 all-gather.5
  98.3 106.9 all-gather.7
  213.0 57.8 all-gather.9
  343.0 117.3 reduce-scatter.8
  602.1 33.1 reduce-scatter.4
  638.1 63.5 reduce-scatter.10
  704.5 68.1 reduce-scatter.6
where the time goes:
time: 844 us; the launch traced here: 832 us
  waiting for transfers between devices  386 us (46%)
  matrix products  148 us (18%)
  starting transfers between devices  80.5 us (10%)
  Pallas kernels  68.5 us (8%)
  other arithmetic  62.9 us (7%)
  local copies, waits for them, and re-layouts  54 us (6%)
  blocking collectives  15.8 us (2%)
  between operations  15.7 us (2%)
    ppermute x72, waiting for transfers between devices, swap(): return lax.ppermute(value, 'seq', [(i, i ^ mask) for i in range(n)])  232 us
    reduce_scatter x4, waiting for transfers between devices, scatter_fsdp(): return lax.psum_scatter(value, 'fsdp', scatter_dimension=0, tiled=True)  141 us
    ppermute x72, starting transfers between devices, swap(): return lax.ppermute(value, 'seq', [(i, i ^ mask) for i in range(n)])  80 us
    unnamed x118, local copies, waits for them, and re-layouts  27 us
    pallas_call x1, Pallas kernels, attend_back(): pl.pallas_call(functools.partial(attend_back_kernel, tile=tile), grid_spe...  26.4 us
    pallas_call x1, Pallas kernels, attend(): pl.pallas_call(functools.partial(attend_kernel, tile=tile), grid_spec=plt...  23.9 us
    pallas_call x3, Pallas kernels, finish(): pl.pallas_call(functools.partial(finish_kernel, n=n, steps=steps, outs=le...  18.2 us
    dot_general x1, matrix products, body(): gate_up_term = dot(h2, d_gate_up, down).astype(bf16)  18.2 us
  transfers between devices with their start and end apart: 80, of which 36 were waited for; matrix products, arithmetic and copies ran while one was open for 25% of the time, Pallas kernels for 8%

commit v1 on v0

--- a/solution.py
+++ b/solution.py
@@ -38,18 +38,29 @@
     return lax.ppermute(value, "seq", [(i, i ^ mask) for i in range(n)])
 
 
+def after(value, first):
+    return lax.optimization_barrier((value, first))[0]
+
+
 def halves(count):
     middle = (count // 2 + 8) // 16 * 16
     return ((0, middle), (middle, count))
 
 
-def gather_streams(value, n):
+def gather_streams(value, n, second=None):
     bits = n.bit_length() - 1
     streams = [{0: value[first:last]} for first, last in halves(value.shape[0])]
     for step in range(bits):
         for index, have in enumerate(streams):
             mask = 1 << ((index + step) % bits)
-            have.update({key ^ mask: swap(item, mask, n) for key, item in have.items()})
+            items = have
+            if step:
+                last = list(have)[-1]
+                items = {k: after(v, have[last]) for k, v in have.items() if k != last}
+                items[last] = have[last]
+                if second is not None:
+                    items = {k: after(v, second) for k, v in items.items()}
+            have.update({key ^ mask: swap(item, mask, n) for key, item in items.items()})
     return [[have[j] for j in range(n)] for have in streams]
 
 
@@ -256,6 +267,71 @@
     )(slot, query, key, value, d_mixed, lse, *tables)
 
 
+def feed_kernel(h_ref, w_ref, both_ref, act_ref):
+    units = act_ref.shape[1]
+    both = jnp.dot(h_ref[...], w_ref[...], preferred_element_type=f32)
+    both_ref[...] = both
+    gate = both[:, :units]
+    act_ref[...] = (gate * jax.nn.sigmoid(gate) * both[:, units:]).astype(bf16)
+
+
+def feed(h2, weight, tile=256):
+    tokens, width = h2.shape
+    units = weight.shape[1] // 2
+    return pl.pallas_call(
+        feed_kernel,
+        grid=(tokens // tile,),
+        in_specs=[
+            pl.BlockSpec((tile, width), lambda i: (i, 0)),
+            pl.BlockSpec((width, 2 * units), lambda i: (0, 0)),
+        ],
+        out_specs=[
+            pl.BlockSpec((tile, 2 * units), lambda i: (i, 0)),
+            pl.BlockSpec((tile, units), lambda i: (i, 0)),
+        ],
+        out_shape=[
+            jax.ShapeDtypeStruct((tokens, 2 * units), f32),
+            jax.ShapeDtypeStruct((tokens, units), bf16),
+        ],
+        cost_estimate=pl.CostEstimate(
+            flops=4 * tokens * width * units, transcendentals=tokens * units,
+            bytes_accessed=2 * tokens * width + 4 * width * units + 10 * tokens * units),
+        name="feed",
+    )(h2, weight)
+
+
+def feed_back_kernel(d_ref, w_ref, both_ref, out_ref):
+    units = w_ref.shape[0]
+    d_act = lax.dot_general(d_ref[...], w_ref[...], (((1,), (1,)), ((), ())),
+                            preferred_element_type=f32)
+    gate, upward = both_ref[:, :units], both_ref[:, units:]
+    sigmoid = jax.nn.sigmoid(gate)
+    out_ref[:, :units] = (
+        d_act * upward * sigmoid * (1.0 + gate * (1.0 - sigmoid))
+    ).astype(bf16)
+    out_ref[:, units:] = (d_act * gate * sigmoid).astype(bf16)
+
+
+def feed_back(d_branch, weight, both, tile=256):
+    tokens, width = d_branch.shape
+    units = weight.shape[0]
+    return pl.pallas_call(
+        feed_back_kernel,
+        grid=(tokens // tile,),
+        in_specs=[
+            pl.BlockSpec((tile, width), lambda i: (i, 0)),
+            pl.BlockSpec((units, width), lambda i: (0, 0)),
+            pl.BlockSpec((tile, 2 * units), lambda i: (i, 0)),
+        ],
+        out_specs=pl.BlockSpec((tile, 2 * units), lambda i: (i, 0)),
+        out_shape=jax.ShapeDtypeStruct((tokens, 2 * units), bf16),
+        cost_estimate=pl.CostEstimate(
+            flops=2 * tokens * width * units, transcendentals=tokens * units,
+            bytes_accessed=2 * tokens * width + 2 * width * units + 12 * tokens * units),
+        name="feed_back",
+    )(d_branch, weight, both)
+
+
 def finish_kernel(s_ref, *refs, n, steps, outs, place):
     ins, out_refs = refs[:-outs], refs[-outs:]
     for stream in range(len(ins) // n):
@@ -267,9 +343,10 @@
             place([choose(s_ref[0], [got[i ^ k] for i in range(n)]) for k in range(n)], out_refs)
 
 
-def finish(s, streams, widths, place, tile):
+def finish(s, streams, widths, place, tile, count=None):
     n = len(streams[0])
-    count, columns = streams[0][0].shape
+    columns = streams[0][0].shape[1]
+    count = count or streams[0][0].shape[0]
     steps = count // tile
     rows = count * len(streams)
     specs = []
@@ -366,10 +443,11 @@
     slot = jnp.sum(jnp.where(blocks[None, :] == ids[:, None], ids[None, :], 0), axis=1)
     tables = rope_tables(tokens)
 
+    d_own = cotangent[0]
+    d_branch = jnp.concatenate(spread_seq(d_own, n), axis=0)
+
     def gather_fsdp(value):
         return lax.all_gather(value, "fsdp", axis=0, tiled=True)
-
-    after = lambda value, first: lax.optimization_barrier((value, first))[0]
 
     small = jnp.concatenate([first_gain, first_bias, second_gain, second_bias, qkv_bias])
     small = lax.all_gather(small, "fsdp", axis=0)
@@ -414,7 +492,7 @@
     core = lax.axis_index("fsdp") % 2
     half = width // 2
     w_out_half = choose(core, [w_first[:half, 3 * part :], w_first[half:, 3 * part :]])
-    w_out_pieces = gather_seq(after(w_out_half, h1), n)
+    w_out_pieces = spread_seq(after(w_out_half, h1), n)
     bias_part = choose(s, [bias_qkv[:, i * part : (i + 1) * part] for i in range(n)])
     projected = jnp.dot(h1, w_qkv, preferred_element_type=f32)
     projected = projected + bias_part.reshape(3 * part)
@@ -444,12 +522,8 @@
 
     normed_two, inverse_two = normalize(residual)
     h2 = jnp.concatenate(gather_seq((normed_two * gain_two + bias_two).astype(bf16), n), axis=0)
-    d_own = cotangent[0]
-    d_branch = jnp.concatenate(gather_seq(after(d_own, h2), n), axis=0)
-    gate = jnp.dot(h2, w_gate_up, preferred_element_type=f32)
-    gate, upward = gate[:, :units], gate[:, units:]
-    sigmoid = jax.nn.sigmoid(gate)
-    activated = (gate * sigmoid * upward).astype(bf16)
+    gate_up, activated = feed(h2, w_gate_up)
+
     across = (((1,), (1,)), ((), ()))
     down = (((0,), (0,)), ((), ()))
     dot = functools.partial(lax.dot_general, preferred_element_type=f32)
@@ -459,18 +533,11 @@
 
     down_term = dot(activated, d_branch, down).astype(bf16)
     down_grad = scatter_fsdp(down_term)
-    mixed_all = jnp.concatenate(gather_seq(after(mixed, d_branch), n), axis=0)
+    mixed_all = jnp.concatenate(spread_seq(after(mixed, h2), n), axis=0)
     branch = dot(after(activated, down_term), w_down, (((1,), (0,)), ((), ())))
-    d_activated = dot(after(d_branch, branch), w_down, across)
+    d_gate_up = feed_back(after(d_branch, branch), w_down, gate_up)
     branch = collect_seq([branch[j * own : (j + 1) * own] for j in range(n)], n)
     block_out = (residual + branch).astype(bf16)
-    d_gate_up = jnp.concatenate(
-        [
-            (d_activated * upward * sigmoid * (1.0 + gate * (1.0 - sigmoid))).astype(bf16),
-            (d_activated * gate * sigmoid).astype(bf16),
-        ],
-        axis=1,
-    )
     gate_up_term = dot(h2, d_gate_up, down).astype(bf16)
     gate_up_grad = scatter_fsdp(gate_up_term)
     d_h2 = dot(after(d_gate_up, gate_up_term), w_gate_up, across)
@@ -519,7 +586,7 @@
     out_grad = scatter_fsdp(out_term.reshape(fs * (rows + extra), part))
 
     down_total = jnp.stack(natural(down_pieces)).reshape(shard, width).astype(f32)
-    gate_up_pieces = gather_streams(after(gate_up_grad, d_h1), n)
+    gate_up_pieces = gather_streams(after(gate_up_grad, qkv_term), n, d_h1)
     gate_total, up_total = finish(
         s, gate_up_pieces, (ffn, ffn),
         functools.partial(place_units, fs), min(64, rows // 2))
@@ -527,10 +594,10 @@
     (qkv_total,) = finish(
         s, qkv_pieces, (3 * width,),
         functools.partial(place_columns, 3), min(64, rows // 2))
-    out_pieces = spread_seq(out_grad, n)
+    out_pieces = spread_seq(after(out_grad, qkv_pieces[1][n - 1]), n)
     (out_total,) = finish(
-        s, [[got[:rows] for got in out_pieces]], (width,),
-        functools.partial(place_columns, 1), rows)
+        s, [out_pieces], (width,),
+        functools.partial(place_columns, 1), rows, rows)
     sums = sum(got[rows:].astype(f32) for got in out_pieces).reshape(extra * part)
     return (
         block_out[None],

time: 844 us -> 793 us (0.940)
  Pallas kernels: 68.5 us -> 102 us
  local copies, waits for them, and re-layouts: 54 us -> 28.4 us
  waiting for transfers between devices: 386 us -> 362 us
  matrix products: 148 us -> 128 us
  starting transfers between devices: 80.5 us -> 66.3 us
    reduce_scatter x4, waiting for transfers between devices: 141 us -> 0.03 us  [scatter_fsdp(): return lax.psum_scatter(value, 'fsdp', scatter_dimension=0, tiled=True)]
    ppermute x72 -> x63, waiting for transfers between devices: 232 us -> 356 us  [swap(): return lax.ppermute(value, 'seq', [(i, i ^ mask) for i in range(n)])]
    pallas_call x0 -> x2, Pallas kernels: none -> 33.5 us  [the longest x1 19.1 us: feed(): pl.pallas_call(feed_kernel, grid=(tokens // tile,), in_specs=[pl.BlockSpe...]
    dot_general x2 -> x0, matrix products: 30 us -> none  [the longest x1 17.4 us: body(): gate = jnp.dot(h2, w_gate_up, preferred_element_type=f32)]
    unnamed x118 -> x99, local copies, waits for them, and re-layouts: 27 us -> 11.8 us
    ppermute x72 -> x63, starting transfers between devices: 80 us -> 66 us  [swap(): return lax.ppermute(value, 'seq', [(i, i ^ mask) for i in range(n)])]
  transfers between devices with their start and end apart: 80 -> 71, of which waited for: 36 -> 36; matrix products, arithmetic and copies ran while one was open for 25% -> 23% of each run, Pallas kernels for 8% -> 11%
where the time goes in v1:
time: 793 us; the launch traced here: 782 us
  waiting for transfers between devices  362 us (46%)
  matrix products  128 us (16%)
  Pallas kernels  102 us (13%)
  starting transfers between devices  66.3 us (8%)
  other arithmetic  63.4 us (8%)
  local copies, waits for them, and re-layouts  28.4 us (4%)
  blocking collectives  15.8 us (2%)
  between operations  15.4 us (2%)
    ppermute x63, waiting for transfers between devices, swap(): return lax.ppermute(value, 'seq', [(i, i ^ mask) for i in range(n)])  356 us
    ppermute x63, starting transfers between devices, swap(): return lax.ppermute(value, 'seq', [(i, i ^ mask) for i in range(n)])  66 us
    pallas_call x1, Pallas kernels, attend_back(): pl.pallas_call(functools.partial(attend_back_kernel, tile=tile), grid_spe...  26.4 us
    pallas_call x1, Pallas kernels, attend(): pl.pallas_call(functools.partial(attend_kernel, tile=tile), grid_spec=plt...  24.1 us
    dot_general x1, matrix products, body(): d_h2 = dot(after(d_gate_up, gate_up_term), w_gate_up, across)  19.4 us
    pallas_call x1, Pallas kernels, feed(): pl.pallas_call(feed_kernel, grid=(tokens // tile,), in_specs=[pl.BlockSpe...  19.1 us
    pallas_call x3, Pallas kernels, finish(): pl.pallas_call(functools.partial(finish_kernel, n=n, steps=steps, outs=le...  18.4 us
    dot_general x1, matrix products, body(): gate_up_term = dot(h2, d_gate_up, down).astype(bf16)  18.2 us
  transfers between devices with their start and end apart: 71, of which 36 were waited for; matrix products, arithmetic and copies ran while one was open for 23% of the time, Pallas kernels for 11%

profile of v1, /device:TPU:0, one launch (start us, length us, event | category | flops | bytes accessed | tf_op | source)
XLA Modules:
  0.0 782.4 jit_solution(17875498815147558550)
XLA Ops:
  12.2 15.8 %all-gather.1 = bf16[8,1,1792]{2,1,0:T(2,128)(2,1)S(1)} all-gather(bf16[1,1,1792]{2,1,0:T(2,128)(2,1)S(1)} %reshape.237), channel_id=2, replica_groups=mesh['seq'=4,'fsdp'=8] {'fsdp'}, dimensions={0}, use_global_device_ids=true | all-gather | bytes 32256 | tf_op jit(solution)/shard_map/all_gather | solution.py:453
  51.7 11.4 %collective-permute-done.1 = bf16[128,2048]{1,0:T(8,128)(2,1)S(1)} collective-permute-done((bf16[128,2048]{1,0:T(8,128)(2,1)}, bf16[128,2048]{1,0:T(8,128)(2,1)S(1)}, u32[]{:S(2)}, u32[]{:S(2)}) %collective-permute-start.1) | collective-permute-done | bytes 524320 | tf_op jit(solution)/shard_map/ppermute | solution.py:38
  104.3 19.7 %collective-permute-done.11 = bf16[1024,512]{1,0:T(8,128)(2,1)S(1)} collective-permute-done((bf16[1024,512]{1,0:T(8,128)(2,1)S(1)}, bf16[1024,512]{1,0:T(8,128)(2,1)S(1)}, u32[]{:S(2)}, u32[]{:S(2)}) %collective-permute-start.11) | collective-permute-done | bytes 1048608 | tf_op jit(solution)/shard_map/ppermute | solution.py:38
  124.0 23.0 %collective-permute-done.10 = bf16[1024,512]{1,0:T(8,128)(2,1)} collective-permute-done((bf16[1024,512]{1,0:T(8,128)(2,1)S(1)}, bf16[1024,512]{1,0:T(8,128)(2,1)}, u32[]{:S(2)}, u32[]{:S(2)}) %collective-permute-start.10) | collective-permute-done | bytes 1048608 | tf_op jit(solution)/shard_map/ppermute | solution.py:38
  155.7 11.7 %fusion.8.q_ref.k_ref.v_ref = f32[1024,1536]{1,0:T(8,128)} fusion(bf16[1024,2048]{1,0:T(8,128)(2,1)} %constant_dynamic-update-slice_fusion, bf16[2048,2048]{1,0:T(8,128)(2,1)} %all-gather.6.cloned.1.call-done, f32[1536]{0:T(1024)S(1)} %add.208), kind=kOutput, calls=%fused_computation.13 | convolution fusion | flops 6444023808 | bytes 16783360 | tf_op jit(solution)/shard_map/dot_general | solution.py:497
  167.5 24.1 %attend.1 = (bf16[1024,512]{1,0:T(8,128)(2,1)}, f32[4,1024,2]{2,1,0:T(8,128)}, bf16[1024,512]{1,0:T(8,128)(2,1)}, bf16[1024,512]{1,0:T(8,128)(2,1)}, bf16[1024,512]{1,0:T(8,128)(2,1)}) custom-call(s32[8]{0:T(128)} %select_reduce_fusion.slot_ref, f32[1024,1536]{1,0:T(8,128)} %fusion.8.q_ref.k_ref.v_ref, f32[1024,1536]{1,0:T(8,128)} %fusion.8.q_ref.k_ref.v_ref, ...), custom_call_target="tpu_custom_call" | custom-call | flops 2147483648 | bytes 12582912 | tf_op jit(solution)/shard_map/attend/pallas_call | solution.py:167
  221.9 42.3 %collective-permute-done.14 = bf16[128,2048]{1,0:T(8,128)(2,1)S(1)} collective-permute-done((bf16[128,2048]{1,0:T(8,128)(2,1)S(1)}, bf16[128,2048]{1,0:T(8,128)(2,1)S(1)}, u32[]{:S(2)}, u32[]{:S(2)}) %collective-permute-start.14) | collective-permute-done | bytes 524320 | tf_op jit(solution)/shard_map/ppermute | solution.py:38
  291.9 19.1 %feed.1 = (f32[1024,2816]{1,0:T(8,128)}, bf16[1024,1408]{1,0:T(8,128)(2,1)}) custom-call(bf16[1024,2048]{1,0:T(8,128)(2,1)} %constant_dynamic-update-slice_fusion.7.h_ref, bf16[2048,2816]{1,0:T(8,128)(2,1)} %all-gather.8.cloned.1.call-done.w_ref), custom_call_target="tpu_custom_call" | custom-call | flops 11811160064 | bytes 30146560 | tf_op jit(solution)/shard_map/feed/pallas_call | solution.py:281
  321.5 12.3 %fusion.117 = (bf16[1024,2048]{1,0:T(8,128)(2,1)}, f32[1024,2048]{1,0:T(8,128)}) fusion(bf16[1024,1408]{1,0:T(8,128)(2,1)} %get-tuple-element.53, bf16[1408,2048]{1,0:T(8,128)(2,1)} %all-gather.10.cloned.1.call-done.w_ref), kind=kOutput, calls=%fused_computation.241 | convolution fusion | flops 5907677184 | bytes 21233664 | tf_op jit(solution)/shard_map/dot_general | solution.py:537
  333.8 14.4 %feed_back.1 = bf16[1024,2816]{1,0:T(8,128)(2,1)} custom-call(bf16[1024,2048]{1,0:T(8,128)(2,1)} %pad_maximum_fusion.1.d_ref, bf16[1408,2048]{1,0:T(8,128)(2,1)} %all-gather.10.cloned.1.call-done.w_ref, f32[1024,2816]{1,0:T(8,128)} %get-tuple-element.55.both_ref), custom_call_target="tpu_custom_call" | custom-call | flops 5905580032 | bytes 27262976 | tf_op jit(solution)/shard_map/feed_back/pallas_call | solution.py:318
  348.2 18.2 %convolution_convert_fusion = bf16[2048,2816]{1,0:T(8,128)(2,1)} fusion(bf16[1024,2048]{1,0:T(8,128)(2,1)} %constant_dynamic-update-slice_fusion.7.h_ref, bf16[1024,2816]{1,0:T(8,128)(2,1)} %feed_back.1), kind=kOutput, calls=%fused_computation.5 | convolution fusion | flops 11816927232 | bytes 21495808 | tf_op jit(solution)/shard_map/dot_general | solution.py:541
  367.0 19.4 %fusion.116 = (bf16[1024,2048]{1,0:T(8,128)(2,1)}, f32[1024,2048]{1,0:T(8,128)S(1)}) fusion(bf16[1024,2816]{1,0:T(8,128)(2,1)} %feed_back.1, bf16[2048,2816]{1,0:T(8,128)(2,1)} %all-gather.8.cloned.1.call-done.w_ref), kind=kOutput, calls=%fused_computation.240 | convolution fusion | flops 11813257216 | bytes 29884416 | tf_op jit(solution)/shard_map/dot_general | solution.py:543
  390.4 12.7 %collective-permute-done.26 = bf16[128,2048]{1,0:T(8,128)(2,1)S(1)} collective-permute-done((bf16[128,2048]{1,0:T(8,128)(2,1)S(1)}, bf16[128,2048]{1,0:T(8,128)(2,1)S(1)}, u32[]{:S(2)}, u32[]{:S(2)}) %collective-permute-start.26) | collective-permute-done | bytes 524320 | tf_op jit(solution)/shard_map/ppermute | solution.py:38
  434.6 17.2 %collective-permute-done.22 = bf16[256,2048]{1,0:T(8,128)(2,1)S(1)} collective-permute-done((bf16[256,2048]{1,0:T(8,128)(2,1)S(1)}, bf16[256,2048]{1,0:T(8,128)(2,1)S(1)}, u32[]{:S(2)}, u32[]{:S(2)}) %collective-permute-start.22) | collective-permute-done | bytes 1048608 | tf_op jit(solution)/shard_map/ppermute | solution.py:38
  451.8 17.4 %collective-permute-done.24 = bf16[256,2048]{1,0:T(8,128)(2,1)S(1)} collective-permute-done((bf16[256,2048]{1,0:T(8,128)(2,1)S(1)}, bf16[256,2048]{1,0:T(8,128)(2,1)S(1)}, u32[]{:S(2)}, u32[]{:S(2)}) %collective-permute-start.24) | collective-permute-done | bytes 1048608 | tf_op jit(solution)/shard_map/ppermute | solution.py:38
  495.4 26.4 %attend_back.1 = bf16[1024,1536]{1,0:T(8,128)(2,1)} custom-call(s32[8]{0:T(128)} %select_reduce_fusion.slot_ref, bf16[1024,512]{1,0:T(8,128)(2,1)} %get-tuple-element.57.q_ref, bf16[1024,512]{1,0:T(8,128)(2,1)} %get-tuple-element.58.k_ref, bf16[1024,512]{1,0:T(8,128)(2,1)} %get-tuple-element.59.v_ref, bf16[1024,512]{1,0:T(8,128)(2,1)} %pad_maximum_fusion.8.d_ref, ...), custom_call_target="tpu_custom_call" | custom-call | flops 5368709120 | bytes 8388608 | tf_op jit(solution)/shard_map/attend_back/pallas_call | solution.py:250
  521.8 11.5 %convolution_convert_fusion.1 = bf16[2048,1536]{1,0:T(8,128)(2,1)} fusion(bf16[1024,2048]{1,0:T(8,128)(2,1)} %constant_dynamic-update-slice_fusion, bf16[1024,1536]{1,0:T(8,128)(2,1)} %attend_back.1), kind=kOutput, calls=%fused_computation.6 | convolution fusion | flops 6445596672 | bytes 13631488 | tf_op jit(solution)/shard_map/dot_general | solution.py:560
  535.1 12.1 %fusion.118 = (bf16[1024,2048]{1,0:T(8,128)(2,1)S(1)}, f32[1024,2048]{1,0:T(8,128)}) fusion(bf16[1024,1536]{1,0:T(8,128)(2,1)} %attend_back.1, bf16[2048,2048]{1,0:T(8,128)(2,1)} %all-gather.6.cloned.1.call-done), kind=kOutput, calls=%fused_computation.242 | convolution fusion | flops 6444548096 | bytes 22020096 | tf_op jit(solution)/shard_map/dot_general | solution.py:563
  555.1 12.6 %collective-permute-done.35 = bf16[128,2048]{1,0:T(8,128)(2,1)S(1)} collective-permute-done((bf16[128,2048]{1,0:T(8,128)(2,1)}, bf16[128,2048]{1,0:T(8,128)(2,1)S(1)}, u32[]{:S(2)}, u32[]{:S(2)}) %collective-permute-start.35) | collective-permute-done | bytes 524320 | tf_op jit(solution)/shard_map/ppermute | solution.py:38
  573.1 25.8 %collective-permute-done.34 = bf16[128,2048]{1,0:T(8,128)(2,1)S(1)} collective-permute-done((bf16[128,2048]{1,0:T(8,128)(2,1)}, bf16[128,2048]{1,0:T(8,128)(2,1)S(1)}, u32[]{:S(2)}, u32[]{:S(2)}) %collective-permute-start.34) | collective-permute-done | bytes 524320 | tf_op jit(solution)/shard_map/ppermute | solution.py:38
  634.1 15.5 %collective-permute-done.46.refs_1_ = bf16[128,2816]{1,0:T(8,128)(2,1)S(1)} collective-permute-done((bf16[128,2816]{1,0:T(8,128)(2,1)}, bf16[128,2816]{1,0:T(8,128)(2,1)S(1)}, u32[]{:S(2)}, u32[]{:S(2)}) %collective-permute-start.46) | collective-permute-done | bytes 720928 | tf_op jit(solution)/shard_map/ppermute | solution.py:38
  655.1 26.8 %collective-permute-done.47.refs_3_ = bf16[128,2816]{1,0:T(8,128)(2,1)} collective-permute-done((bf16[128,2816]{1,0:T(8,128)(2,1)S(1)}, bf16[128,2816]{1,0:T(8,128)(2,1)}, u32[]{:S(2)}, u32[]{:S(2)}) %collective-permute-start.47) | collective-permute-done | bytes 720928 | tf_op jit(solution)/shard_map/ppermute | solution.py:38
  683.9 15.7 %collective-permute-done.58.refs_6_ = bf16[128,2816]{1,0:T(8,128)(2,1)} collective-permute-done((bf16[128,2816]{1,0:T(8,128)(2,1)}, bf16[128,2816]{1,0:T(8,128)(2,1)}, u32[]{:S(2)}, u32[]{:S(2)}) %collective-permute-start.58) | collective-permute-done | bytes 720928 | tf_op jit(solution)/shard_map/ppermute | solution.py:38
  726.4 16.7 %collective-permute-done.49.refs_7_ = bf16[128,1536]{1,0:T(8,128)(2,1)S(1)} collective-permute-done((bf16[128,1536]{1,0:T(8,128)(2,1)S(1)}, bf16[128,1536]{1,0:T(8,128)(2,1)S(1)}, u32[]{:S(2)}, u32[]{:S(2)}) %collective-permute-start.49) | collective-permute-done | bytes 393248 | tf_op jit(solution)/shard_map/ppermute | solution.py:38
  (333 shorter events, 325.0 us)
Async XLA Ops:
  7.2 89.0 %all-gather.6.cloned.1.call-start = ((), (), s32[]{:S(2)}) async-start(), calls=%async_computation.4 | async-start | bytes 9437184 | tf_op jit(solution)/shard_map/all_gather | solution.py:450
  11.2 280.7 %all-gather.8.cloned.1.call-start = ((), (), s32[]{:S(2)}) async-start(), calls=%async_computation.5 | async-start | bytes 12976128 | tf_op jit(solution)/shard_map/all_gather | solution.py:450
  47.3 274.2 %all-gather.10.cloned.1.call-start = ((), (), s32[]{:S(2)}) async-start(), calls=%async_computation.6 | async-start | bytes 6488064 | tf_op jit(solution)/shard_map/all_gather | solution.py:450
  99.4 47.6 %collective-permute-start.10 = (bf16[1024,512]{1,0:T(8,128)(2,1)S(1)}, bf16[1024,512]{1,0:T(8,128)(2,1)}, u32[]{:S(2)}, u32[]{:S(2)}) collective-permute-start(bf16[1024,512]{1,0:T(8,128)(2,1)S(1)} %slice_select_fusion), channel_id=1, source_target_pairs={{0,16},{8,24},{16,0},{24,8},{1,17},{9,25},{17,1},{25,9},{2,18},{10... | collective-permute-start | bytes 3145736 | tf_op jit(solution)/shard_map/ppermute | solution.py:38
  100.9 46.1 %collective-permute-start.9 = (bf16[1024,512]{1,0:T(8,128)(2,1)S(1)}, bf16[1024,512]{1,0:T(8,128)(2,1)}, u32[]{:S(2)}, u32[]{:S(2)}) collective-permute-start(bf16[1024,512]{1,0:T(8,128)(2,1)S(1)} %slice_select_fusion), channel_id=1, source_target_pairs={{0,24},{8,16},{16,8},{24,0},{1,25},{9,17},{17,9},{25,1},{2,26},{10... | collective-permute-start | bytes 3145736 | tf_op jit(solution)/shard_map/ppermute | solution.py:38
  104.2 526.4 %reduce-scatter.9.cloned.1.call-start = ((), (), s32[]{:S(2)}) async-start(), calls=%async_computation.9 | async-start | bytes 12976128 | tf_op jit(solution)/shard_map/reduce_scatter | solution.py:532
  151.5 58.7 %collective-permute-start.12 = (bf16[1024,2048]{1,0:T(8,128)(2,1)}, bf16[1024,2048]{1,0:T(8,128)(2,1)}, u32[]{:S(2)}, u32[]{:S(2)}) collective-permute-start(bf16[1024,2048]{1,0:T(8,128)(2,1)} %pad_maximum_fusion), channel_id=1, source_target_pairs={{0,1},{1,0},{2,3},{3,2},{4,5},{5,4},{6,7},{7,6},{8,9},{9,8},{10,11... | collective-permute-start | bytes 12582920 | tf_op jit(solution)/shard_map/ppermute | solution.py:514
  196.3 69.9 %collective-permute-start.21 = (bf16[256,2048]{1,0:T(8,128)(2,1)}, bf16[256,2048]{1,0:T(8,128)(2,1)}, u32[]{:S(2)}, u32[]{:S(2)}) collective-permute-start(bf16[256,2048]{1,0:T(8,128)(2,1)} %bitcast.3), channel_id=1, source_target_pairs={{0,24},{8,16},{16,8},{24,0},{1,25},{9,17},{17,9},{25,1},{2,26},{10... | collective-permute-start | bytes 3145736 | tf_op jit(solution)/shard_map/ppermute | solution.py:38
  202.9 63.3 %collective-permute-start.20 = (bf16[256,2048]{1,0:T(8,128)(2,1)}, bf16[256,2048]{1,0:T(8,128)(2,1)S(1)}, u32[]{:S(2)}, u32[]{:S(2)}) collective-permute-start(bf16[256,2048]{1,0:T(8,128)(2,1)} %bitcast.3), channel_id=1, source_target_pairs={{0,16},{8,24},{16,0},{24,8},{1,17},{9,25},{17,1},{25,9},{2,18},{10... | collective-permute-start | bytes 3145736 | tf_op jit(solution)/shard_map/ppermute | solution.py:38
  208.5 57.7 %collective-permute-start.19 = (bf16[256,2048]{1,0:T(8,128)(2,1)}, bf16[256,2048]{1,0:T(8,128)(2,1)S(1)}, u32[]{:S(2)}, u32[]{:S(2)}) collective-permute-start(bf16[256,2048]{1,0:T(8,128)(2,1)} %bitcast.3), channel_id=1, source_target_pairs={{0,8},{8,0},{16,24},{24,16},{1,9},{9,1},{17,25},{25,17},{2,10},{10... | collective-permute-start | bytes 3145736 | tf_op jit(solution)/shard_map/ppermute | solution.py:38
  219.6 44.6 %collective-permute-start.14 = (bf16[128,2048]{1,0:T(8,128)(2,1)S(1)}, bf16[128,2048]{1,0:T(8,128)(2,1)S(1)}, u32[]{:S(2)}, u32[]{:S(2)}) collective-permute-start(bf16[128,2048]{1,0:T(8,128)(2,1)S(1)} %get-tuple-element.49), channel_id=1, source_target_pairs={{0,16},{8,24},{16,0},{24,8},{1,17},{9,25},{17,1},{25,9},{2,18},{10... | collective-permute-start | bytes 1572872 | tf_op jit(solution)/shard_map/ppermute | solution.py:38
  221.0 44.4 %collective-permute-start.13 = (bf16[128,2048]{1,0:T(8,128)(2,1)S(1)}, bf16[128,2048]{1,0:T(8,128)(2,1)S(1)}, u32[]{:S(2)}, u32[]{:S(2)}) collective-permute-start(bf16[128,2048]{1,0:T(8,128)(2,1)S(1)} %get-tuple-element.50), channel_id=1, source_target_pairs={{0,8},{8,0},{16,24},{24,16},{1,9},{9,1},{17,25},{25,17},{2,10},{10... | collective-permute-start | bytes 1572872 | tf_op jit(solution)/shard_map/ppermute | solution.py:38
  366.4 285.2 %reduce-scatter.11.cloned.1.call-start = ((), (), s32[]{:S(2)}) async-start(), calls=%async_computation.10 | async-start | bytes 6488064 | tf_op jit(solution)/shard_map/reduce_scatter | solution.py:532
  367.0 288.1 %reduce-scatter.7.cloned.1.call-start = ((), (), s32[]{:S(2)}) async-start(), calls=%async_computation.8 | async-start | bytes 7077888 | tf_op jit(solution)/shard_map/reduce_scatter | solution.py:532
  420.3 48.9 %collective-permute-start.24 = (bf16[256,2048]{1,0:T(8,128)(2,1)S(1)}, bf16[256,2048]{1,0:T(8,128)(2,1)S(1)}, u32[]{:S(2)}, u32[]{:S(2)}) collective-permute-start(bf16[256,2048]{1,0:T(8,128)(2,1)S(1)} %get-tuple-element.113), channel_id=1, source_target_pairs={{0,24},{8,16},{16,8},{24,0},{1,25},{9,17},{17,9},{25,1},{2,26},{10... | collective-permute-start | bytes 3145736 | tf_op jit(solution)/shard_map/ppermute | solution.py:38
  422.3 46.9 %collective-permute-start.23 = (bf16[256,2048]{1,0:T(8,128)(2,1)S(1)}, bf16[256,2048]{1,0:T(8,128)(2,1)S(1)}, u32[]{:S(2)}, u32[]{:S(2)}) collective-permute-start(bf16[256,2048]{1,0:T(8,128)(2,1)S(1)} %get-tuple-element.114), channel_id=1, source_target_pairs={{0,16},{8,24},{16,0},{24,8},{1,17},{9,25},{17,1},{25,9},{2,18},{10... | collective-permute-start | bytes 3145736 | tf_op jit(solution)/shard_map/ppermute | solution.py:38
  533.3 211.6 %reduce-scatter.5.cloned.1.call-start = ((), (), s32[]{:S(2)}) async-start(), calls=%async_computation.7 | async-start | bytes 2506752 | tf_op jit(solution)/shard_map/reduce_scatter | solution.py:532
  549.3 55.2 %collective-permute-start.41 = (bf16[256,2048]{1,0:T(8,128)(2,1)S(1)}, bf16[256,2048]{1,0:T(8,128)(2,1)}, u32[]{:S(2)}, u32[]{:S(2)}) collective-permute-start(bf16[256,2048]{1,0:T(8,128)(2,1)S(1)} %pad_maximum_fusion.9), channel_id=1, source_target_pairs={{0,16},{8,24},{16,0},{24,8},{1,17},{9,25},{17,1},{25,9},{2,18},{10... | collective-permute-start | bytes 3145736 | tf_op jit(solution)/shard_map/ppermute | solution.py:38
  550.6 54.7 %collective-permute-start.40 = (bf16[256,2048]{1,0:T(8,128)(2,1)S(1)}, bf16[256,2048]{1,0:T(8,128)(2,1)}, u32[]{:S(2)}, u32[]{:S(2)}) collective-permute-start(bf16[256,2048]{1,0:T(8,128)(2,1)S(1)} %pad_maximum_fusion.9), channel_id=1, source_target_pairs={{0,8},{8,0},{16,24},{24,16},{1,9},{9,1},{17,25},{25,17},{2,10},{10... | collective-permute-start | bytes 3145736 | tf_op jit(solution)/shard_map/ppermute | solution.py:38
  551.0 47.9 %collective-permute-start.34 = (bf16[128,2048]{1,0:T(8,128)(2,1)}, bf16[128,2048]{1,0:T(8,128)(2,1)S(1)}, u32[]{:S(2)}, u32[]{:S(2)}) collective-permute-start(bf16[128,2048]{1,0:T(8,128)(2,1)} %get-tuple-element.104), channel_id=1, source_target_pairs={{0,16},{8,24},{16,0},{24,8},{1,17},{9,25},{17,1},{25,9},{2,18},{10... | collective-permute-start | bytes 1572872 | tf_op jit(solution)/shard_map/ppermute | solution.py:38
  650.1 49.5 %collective-permute-start.58 = (bf16[128,2816]{1,0:T(8,128)(2,1)}, bf16[128,2816]{1,0:T(8,128)(2,1)}, u32[]{:S(2)}, u32[]{:S(2)}) collective-permute-start(bf16[128,2816]{1,0:T(8,128)(2,1)} %get-tuple-element.73.refs_4_), channel_id=1, source_target_pairs={{0,16},{8,24},{16,0},{24,8},{1,17},{9,25},{17,1},{25,9},{2,18},{10... | collective-permute-start | bytes 2162696 | tf_op jit(solution)/shard_map/ppermute | solution.py:38
  651.6 53.6 %collective-permute-start.63 = (bf16[176,2048]{1,0:T(8,128)(2,1)}, bf16[176,2048]{1,0:T(8,128)(2,1)}, u32[]{:S(2)}, u32[]{:S(2)}) collective-permute-start(bf16[176,2048]{1,0:T(8,128)(2,1)} %reduce-scatter.11.cloned.1.call-done), channel_id=1, source_target_pairs={{0,8},{8,0},{16,24},{24,16},{1,9},{9,1},{17,25},{25,17},{2,10},{10... | collective-permute-start | bytes 2162696 | tf_op jit(solution)/shard_map/ppermute | solution.py:38
  652.3 62.7 %collective-permute-start.62 = (bf16[176,2048]{1,0:T(8,128)(2,1)}, bf16[176,2048]{1,0:T(8,128)(2,1)}, u32[]{:S(2)}, u32[]{:S(2)}) collective-permute-start(bf16[176,2048]{1,0:T(8,128)(2,1)} %reduce-scatter.11.cloned.1.call-done), channel_id=1, source_target_pairs={{0,16},{8,24},{16,0},{24,8},{1,17},{9,25},{17,1},{25,9},{2,18},{10... | collective-permute-start | bytes 2162696 | tf_op jit(solution)/shard_map/ppermute | solution.py:38
  653.5 62.0 %collective-permute-start.61 = (bf16[176,2048]{1,0:T(8,128)(2,1)}, bf16[176,2048]{1,0:T(8,128)(2,1)}, u32[]{:S(2)}, u32[]{:S(2)}) collective-permute-start(bf16[176,2048]{1,0:T(8,128)(2,1)} %reduce-scatter.11.cloned.1.call-done), channel_id=1, source_target_pairs={{0,24},{8,16},{16,8},{24,0},{1,25},{9,17},{17,9},{25,1},{2,26},{10... | collective-permute-start | bytes 2162696 | tf_op jit(solution)/shard_map/ppermute | solution.py:38
  (83 other events, 1318.5 us)
Sparse Core Ops, SparseCore 0:
  11.3 84.8 all-gather.5
  98.4 106.4 all-gather.7
  206.6 58.6 all-gather.9
  366.5 117.0 reduce-scatter.8
  486.3 63.2 reduce-scatter.10
  552.3 68.1 reduce-scatter.6
  630.8 34.2 reduce-scatter.4

commit v2 on v1

--- a/solution.py
+++ b/solution.py
@@ -64,30 +64,9 @@
     return [[have[j] for j in range(n)] for have in streams]
 
 
-def gather_seq(value, n):
-    return [jnp.concatenate(pair, axis=0) for pair in zip(*gather_streams(value, n))]
-
-
-def scatter_seq(pieces, n):
-    bits = n.bit_length() - 1
-    streams = [
-        {j: pieces[j][first:last] for j in range(n)}
-        for first, last in halves(pieces[0].shape[0])
-    ]
-    for step in range(bits):
-        for index, have in enumerate(streams):
-            mask = 1 << ((index + bits - 1 - step) % bits)
-            got = {
-                key ^ mask: swap(item.astype(bf16), mask, n)
-                for key, item in have.items()
-                if key & mask
-            }
-            streams[index] = {
-                key: item + got[key].astype(f32)
-                for key, item in have.items()
-                if not key & mask
-            }
-    return jnp.concatenate([have[0] for have in streams], axis=0)
+def gather_seq(value, n, second=None):
+    streams = gather_streams(value, n, second)
+    return [jnp.concatenate(pair, axis=0) for pair in zip(*streams)]
 
 
 def exchange_seq(pieces, n):
@@ -96,11 +75,6 @@
 
 def spread_seq(value, n):
     return exchange_seq([value] * n, n)
-
-
-def collect_seq(pieces, n):
-    got = exchange_seq([pieces[0]] + [piece.astype(bf16) for piece in pieces[1:]], n)
-    return sum(item.astype(f32) for item in got)
 
 
 def choose(index, options):
@@ -108,6 +82,306 @@
     for i, option in enumerate(options[1:], 1):
         out = jnp.where(index == i, option, out)
     return out
+
+
+def flip(s, mask, n):
+    out = 0
+    bit = 1
+    while bit < n:
+        out += bit * ((s // bit + mask // bit) % 2)
+        bit *= 2
+    return out
+
+
+def greet(partners):
+    barrier = pltpu.get_barrier_semaphore()
+    for partner in partners:
+        pl.semaphore_signal(
+            barrier, inc=1, device_id={"seq": partner}, device_id_type=pl.DeviceIdType.MESH
+        )
+    pl.semaphore_wait(barrier, len(partners))
+
+
+def dot_scatter_kernel(
+    a_ref, w_ref, *refs, n, tile, ride
+):
+    if ride:
+        x_ref, out_ref, x_out_ref, *refs, x_sent, x_came, x_local = refs
+    else:
+        out_ref, *refs = refs
+    w_buf, acc, out_buf, in_buf, sent, came, local = refs
+    bits = n.bit_length() - 1
+    s = lax.axis_index("seq")
+    rows = a_ref.shape[0] // n
+    width = w_ref.shape[0]
+    cut = halves(rows)
+
+    def load(i):
+        span = pl.ds(pl.multiple_of(i * tile, tile), tile)
+        return pltpu.make_async_copy(
+            w_ref.at[span, pl.ds(0, a_ref.shape[1])], w_buf.at[span, :], local.at[i])
+
+    for i in range(width // tile):
+        load(i).start()
+    copies = {}
+    if ride:
+        greet([flip(s, j, n) for j in range(1, n)])
+        part = x_out_ref.shape[1]
+        for j in range(1, n):
+            partner = flip(s, j, n)
+            copy = pltpu.make_async_remote_copy(
+                src_ref=x_ref.at[:, pl.ds(pl.multiple_of(partner * part, part), part)],
+                dst_ref=x_out_ref.at[pl.ds(j * rows, rows), :],
+                send_sem=x_sent.at[j], recv_sem=x_came.at[j],
+                device_id={"seq": partner}, device_id_type=pl.DeviceIdType.MESH,
+            )
+            copy.start()
+            copies["ride", j] = copy
+        keep = pltpu.make_async_copy(
+            x_ref.at[:, pl.ds(pl.multiple_of(s * part, part), part)],
+            x_out_ref.at[pl.ds(0, rows), :], x_local)
+        keep.start()
+        keep.wait()
+    else:
+        greet([flip(s, 1 << bit, n) for bit in range(bits)])
+
+    def mask_of(stream, step):
+        return 1 << ((stream + bits - 1 - step) % bits)
+
+    def ship(stream, key, mask):
+        span = pl.ds(cut[stream][0], cut[stream][1] - cut[stream][0])
+        out_buf[key, span, :] = acc[key, span, :].astype(bf16)
+        copy = pltpu.make_async_remote_copy(
+            src_ref=out_buf.at[key, span, :],
+            dst_ref=in_buf.at[key, span, :],
+            send_sem=sent.at[stream, key],
+            recv_sem=came.at[stream, key],
+            device_id={"seq": flip(s, mask, n)},
+            device_id_type=pl.DeviceIdType.MESH,
+        )
+        copy.start()
+        copies[stream, key] = copy
+
+    for key in sorted(range(n), key=lambda k: (-bin(k).count("1"), -k)):
+
+        def columns(i, _, key=key):
+            span = pl.ds(pl.multiple_of(i * tile, tile), tile)
+            if key == n - 1:
+                load(i).wait()
+            acc[key, :, span] = lax.dot_general(
+                a_ref[pl.ds(key * rows, rows), :], w_buf[span, :],
+                (((1,), (1,)), ((), ())), preferred_element_type=f32)
+            return 0
+
+        lax.fori_loop(0, width // tile, columns, 0)
+        for stream in range(2):
+            mask = mask_of(stream, 0)
+            if key & mask:
+                ship(stream, key, mask)
+    have = [list(range(n)), list(range(n))]
+    for step in range(bits):
+        for stream in range(2):
+            mask = mask_of(stream, step)
+            span = pl.ds(cut[stream][0], cut[stream][1] - cut[stream][0])
+            kept = [key for key in have[stream] if not key & mask]
+            if step:
+                for key in have[stream]:
+                    if key & mask:
+                        ship(stream, key, mask)
+            have[stream] = kept
+        for stream in range(2):
+            mask = mask_of(stream, step)
+            span = pl.ds(cut[stream][0], cut[stream][1] - cut[stream][0])
+            for key in have[stream]:
+                copies[stream, key ^ mask].wait_recv()
+                total = acc[key, span, :] + in_buf[key ^ mask, span, :].astype(f32)
+                if step == bits - 1:
+                    out_ref[span, :] = total
+                else:
+                    acc[key, span, :] = total
+    for key, copy in copies.items():
+        copy.wait_send()
+        if key[0] == "ride":
+            copy.wait_recv()
+
+
+def dot_scatter(a, weight, n, collective_id, ride=None, tile=512):
+    rows, depth = a.shape
+    width = weight.shape[0]
+    own = rows // n
+    block = lambda shape: pl.BlockSpec(shape, lambda i: (0, 0))
+    return pl.pallas_call(
+        functools.partial(dot_scatter_kernel, n=n, tile=tile, ride=ride is not None),
+        grid=(1,),
+        in_specs=[block((rows, depth)), pl.BlockSpec(memory_space=pl.ANY)]
+        + ([] if ride is None else [block(ride.shape)]),
+        out_specs=[block((own, width))]
+        + ([] if ride is None else [block((rows, ride.shape[1] // n))]),
+        out_shape=[jax.ShapeDtypeStruct((own, width), f32)]
+        + ([] if ride is None else [jax.ShapeDtypeStruct((rows, ride.shape[1] // n), bf16)]),
+        scratch_shapes=[
+            pltpu.VMEM((width, depth), bf16),
+            pltpu.VMEM((n, own, width), f32),
+            pltpu.VMEM((n, own, width), bf16),
+            pltpu.VMEM((n, own, width), bf16),
+            pltpu.SemaphoreType.DMA((2, n)),
+            pltpu.SemaphoreType.DMA((2, n)),
+            pltpu.SemaphoreType.DMA((width // tile,)),
+        ]
+        + ([] if ride is None else [
+            pltpu.SemaphoreType.DMA((n,)),
+            pltpu.SemaphoreType.DMA((n,)),
+            pltpu.SemaphoreType.DMA(()),
+        ]),
+        compiler_params=pltpu.CompilerParams(
+            collective_id=collective_id, has_side_effects=True),
+        cost_estimate=pl.CostEstimate(
+            flops=2 * rows * depth * width, transcendentals=0,
+            bytes_accessed=40 * rows * width),
+    )(a, weight, *([] if ride is None else [ride]))
+
+
+def pair_dot_kernel(
+    a_ref, b_ref, out_ref, mine, other, out_buf, in_buf, sent, came, local, *, shards, tile
+):
+    me = lax.axis_index("fsdp")
+    core = me % 2
+    partner = me + 1 - 2 * core
+    block = a_ref.shape[0] // shards
+    loads = []
+    for side, (to, parity) in enumerate(((other, 1 - core), (mine, core))):
+        for z in range(shards // 2):
+            first = pl.multiple_of((2 * z + parity) * block, block)
+            load = pltpu.make_async_copy(
+                a_ref.at[pl.ds(first, block), :], to.at[pl.ds(z * block, block), :],
+                local.at[side, z])
+            load.start()
+            loads.append(load)
+    barrier = pltpu.get_barrier_semaphore()
+    pl.semaphore_signal(
+        barrier, inc=1, device_id={"fsdp": partner}, device_id_type=pl.DeviceIdType.MESH
+    )
+    pl.semaphore_wait(barrier, 1)
+    for load in loads:
+        load.wait()
+    steps = b_ref.shape[1] // tile
+    edges = (0, (steps + 1) // 2, steps)
+    copies = []
+    for part in range(2):
+
+        def keep(i, _):
+            cols = pl.ds(pl.multiple_of(i * tile, tile), tile)
+            out_buf[:, cols] = jnp.dot(
+                other[...], b_ref[:, cols], preferred_element_type=f32).astype(bf16)
+            return 0
+
+        lax.fori_loop(edges[part], edges[part + 1], keep, 0)
+        span = pl.ds(edges[part] * tile, (edges[part + 1] - edges[part]) * tile)
+        copy = pltpu.make_async_remote_copy(
+            src_ref=out_buf.at[:, span], dst_ref=in_buf.at[:, span],
+            send_sem=sent.at[part], recv_sem=came.at[part],
+            device_id={"fsdp": partner}, device_id_type=pl.DeviceIdType.MESH,
+        )
+        copy.start()
+        copies.append(copy)
+    for part in range(2):
+        copies[part].wait_recv()
+
+        def add(i, _):
+            cols = pl.ds(pl.multiple_of(i * tile, tile), tile)
+            total = jnp.dot(mine[...], b_ref[:, cols], preferred_element_type=f32)
+            out_ref[:, cols] = (total + in_buf[:, cols].astype(f32)).astype(bf16)
+            return 0
+
+        lax.fori_loop(edges[part], edges[part + 1], add, 0)
+    for copy in copies:
+        copy.wait_send()
+
+
+def pair_dot(turned, b, shards, collective_id):
+    rows, tokens = turned.shape
+    rows //= 2
+    width = b.shape[1]
+    tile = 256 if width % 256 == 0 else 128
+    whole = lambda shape: pl.BlockSpec(shape, lambda i: (0, 0))
+    return pl.pallas_call(
+        functools.partial(pair_dot_kernel, shards=shards, tile=tile),
+        grid=(1,),
+        in_specs=[pl.BlockSpec(memory_space=pl.ANY), whole((tokens, width))],
+        out_specs=whole((rows, width)),
+        out_shape=jax.ShapeDtypeStruct((rows, width), bf16),
+        scratch_shapes=[
+            pltpu.VMEM((rows, tokens), bf16),
+            pltpu.VMEM((rows, tokens), bf16),
+            pltpu.VMEM((rows, width), bf16),
+            pltpu.VMEM((rows, width), bf16),
+            pltpu.SemaphoreType.DMA((2,)),
+            pltpu.SemaphoreType.DMA((2,)),
+            pltpu.SemaphoreType.DMA((2, shards // 2)),
+        ],
+        compiler_params=pltpu.CompilerParams(
+            collective_id=collective_id, has_side_effects=True),
+        cost_estimate=pl.CostEstimate(
+            flops=4 * tokens * rows * width, transcendentals=0,
+            bytes_accessed=10 * tokens * width),
+    )(turned, b)
+
+
+def column_of(group, core, n, part):
+    half = n // 2
+    return pl.multiple_of(((group // half + core) % 2) * half * part + (group % half) * part, part)
+
+
+def exchange_kernel(x_ref, out_ref, sent, came, local, *, n, part, to_columns):
+    s = lax.axis_index("seq")
+    core = lax.axis_index("fsdp") % 2
+    rows = (x_ref if not to_columns else out_ref).shape[0]
+    partners = [flip(s, j, n) for j in range(1, n)]
+    greet(partners)
+    copies = []
+    for j in list(range(1, n)):
+        partner = partners[j - 1]
+        if to_columns:
+            src = x_ref.at[pl.ds(j * rows, rows), :]
+            dst = out_ref.at[:, pl.ds(column_of(s, core, n, part), part)]
+        else:
+            src = x_ref.at[:, pl.ds(column_of(partner, core, n, part), part)]
+            dst = out_ref.at[pl.ds(j * rows, rows), :]
+        copy = pltpu.make_async_remote_copy(
+            src_ref=src, dst_ref=dst, send_sem=sent.at[j], recv_sem=came.at[j],
+            device_id={"seq": partner}, device_id_type=pl.DeviceIdType.MESH,
+        )
+        copy.start()
+        copies.append(copy)
+    own = pl.ds(column_of(s, core, n, part), part)
+    if to_columns:
+        keep = pltpu.make_async_copy(x_ref.at[pl.ds(0, rows), :], out_ref.at[:, own], local)
+    else:
+        keep = pltpu.make_async_copy(x_ref.at[:, own], out_ref.at[pl.ds(0, rows), :], local)
+    keep.start()
+    keep.wait()
+    for copy in copies:
+        copy.wait()
+
+
+def exchange(x, n, part, to_columns, collective_id):
+    rows, width = x.shape
+    shape = (rows // n, n * part) if to_columns else (rows * n, part)
+    return pl.pallas_call(
+        functools.partial(exchange_kernel, n=n, part=part, to_columns=to_columns),
+        in_specs=[pl.BlockSpec(memory_space=pltpu.VMEM)],
+        out_specs=pl.BlockSpec(memory_space=pltpu.VMEM),
+        out_shape=jax.ShapeDtypeStruct(shape, x.dtype),
+        scratch_shapes=[
+            pltpu.SemaphoreType.DMA((n,)),
+            pltpu.SemaphoreType.DMA((n,)),
+            pltpu.SemaphoreType.DMA(()),
+        ],
+        compiler_params=pltpu.CompilerParams(
+            collective_id=collective_id, has_side_effects=True),
+        cost_estimate=pl.CostEstimate(
+            flops=0, transcendentals=0, bytes_accessed=30 * rows * width),
+    )(x)
 
 
 def turn(tensor, cosine, left, right, sign):
@@ -267,10 +541,44 @@
     )(slot, query, key, value, d_mixed, lse, *tables)
 
 
-def feed_kernel(h_ref, w_ref, both_ref, act_ref):
+def project_kernel(h_ref, w_ref, bias_ref, out_ref, turned_ref):
+    out_ref[...] = (
+        jnp.dot(h_ref[...], w_ref[...], preferred_element_type=f32) + bias_ref[...]
+    )
+    turned_ref[...] = jnp.transpose(h_ref[...])
+
+
+def project(h1, weight, bias, tile=256):
+    tokens, width = h1.shape
+    columns = bias.shape[1]
+    return pl.pallas_call(
+        project_kernel,
+        grid=(tokens // tile,),
+        in_specs=[
+            pl.BlockSpec((tile, width), lambda i: (i, 0)),
+            pl.BlockSpec((width, columns), lambda i: (0, 0)),
+            pl.BlockSpec((1, columns), lambda i: (0, 0)),
+        ],
+        out_specs=[
+            pl.BlockSpec((tile, columns), lambda i: (i, 0)),
+            pl.BlockSpec((width, tile), lambda i: (0, i)),
+        ],
+        out_shape=[
+            jax.ShapeDtypeStruct((tokens, columns), f32),
+            jax.ShapeDtypeStruct((width, tokens), bf16),
+        ],
+        cost_estimate=pl.CostEstimate(
+            flops=2 * tokens * width * columns, transcendentals=0,
+            bytes_accessed=4 * tokens * width + 2 * width * columns + 4 * tokens * columns),
+        name="project",
+    )(h1, weight, bias)
+
+
+def feed_kernel(h_ref, w_ref, both_ref, act_ref, turned_ref):
     units = act_ref.shape[1]
     both = jnp.dot(h_ref[...], w_ref[...], preferred_element_type=f32)
     both_ref[...] = both
+    turned_ref[...] = jnp.transpose(h_ref[...])
     gate = both[:, :units]
     act_ref[...] = (gate * jax.nn.sigmoid(gate) * both[:, units:]).astype(bf16)
 
@@ -288,14 +596,16 @@
         out_specs=[
             pl.BlockSpec((tile, 2 * units), lambda i: (i, 0)),
             pl.BlockSpec((tile, units), lambda i: (i, 0)),
+            pl.BlockSpec((width, tile), lambda i: (0, i)),
         ],
         out_shape=[
             jax.ShapeDtypeStruct((tokens, 2 * units), f32),
             jax.ShapeDtypeStruct((tokens, units), bf16),
+            jax.ShapeDtypeStruct((width, tokens), bf16),
         ],
         cost_estimate=pl.CostEstimate(
             flops=4 * tokens * width * units, transcendentals=tokens * units,
-            bytes_accessed=2 * tokens * width + 4 * width * units + 10 * tokens * units),
+            bytes_accessed=4 * tokens * width + 4 * width * units + 10 * tokens * units),
         name="feed",
     )(h2, weight)
 
@@ -425,6 +735,9 @@
     fs,
 ):
     s = lax.axis_index("seq")
+    core = lax.axis_index("fsdp") % 2
+    by_core = lambda a, b: [jnp.where(core == 0, a, b), jnp.where(core == 0, b, a)]
+
     inputs = hidden_in[0].astype(f32)
     own, width = inputs.shape
     part = width // n
@@ -470,7 +783,6 @@
     )
     out_part = choose(s, [out_weight[:, i * part : (i + 1) * part] for i in range(n)])
     w_first = gather_fsdp(jnp.concatenate([qkv_part, out_part], axis=1))
-    w_qkv = w_first[:, : 3 * part]
 
     normed_one, inverse_one = normalize(inputs)
     h1_own = (normed_one * gain_one + bias_one).astype(bf16)
@@ -489,13 +801,11 @@
     w_down = gather_fsdp(choose(s, [down_weight[i * piece : (i + 1) * piece] for i in range(n)]))
 
     h1 = jnp.concatenate(gather_seq(h1_own, n), axis=0)
-    core = lax.axis_index("fsdp") % 2
     half = width // 2
     w_out_half = choose(core, [w_first[:half, 3 * part :], w_first[half:, 3 * part :]])
     w_out_pieces = spread_seq(after(w_out_half, h1), n)
     bias_part = choose(s, [bias_qkv[:, i * part : (i + 1) * part] for i in range(n)])
-    projected = jnp.dot(h1, w_qkv, preferred_element_type=f32)
-    projected = projected + bias_part.reshape(3 * part)
+    projected, h1_turned = project(h1, w_first, bias_part.reshape(1, 3 * part))
     head_out, lse, query, key, value = attend(slot, projected, tables)
 
     def natural(pieces):
@@ -504,70 +814,75 @@
     def to_columns(pieces):
         return jnp.concatenate(natural(pieces), axis=1)
 
-    def column_parts(value):
-        return natural([value[:, k * part : (k + 1) * part] for k in range(n)])
-
-    mixed = to_columns(
-        exchange_seq([head_out[j * own : (j + 1) * own] for j in range(n)], n)
-    )
+    mixed = exchange(head_out, n, part, True, 1)
     w_out = to_columns(w_out_pieces)
     w_out = [w_out, lax.ppermute(w_out, "fsdp", [(i, i ^ 1) for i in range(fs)])]
-    by_core = lambda a, b: [jnp.where(core == 0, a, b), jnp.where(core == 0, b, a)]
-    mixed_first, mixed_second = by_core(mixed[:, :half], mixed[:, half:])
     residual = (
         inputs
-        + jnp.dot(mixed_first, w_out[0], preferred_element_type=f32)
-        + jnp.dot(mixed_second, w_out[1], preferred_element_type=f32)
+        + jnp.dot(mixed[:, :half], w_out[0], preferred_element_type=f32)
+        + jnp.dot(mixed[:, half:], w_out[1], preferred_element_type=f32)
     )
 
     normed_two, inverse_two = normalize(residual)
     h2 = jnp.concatenate(gather_seq((normed_two * gain_two + bias_two).astype(bf16), n), axis=0)
-    gate_up, activated = feed(h2, w_gate_up)
+    gate_up, activated, h2_turned = feed(h2, w_gate_up)
 
     across = (((1,), (1,)), ((), ()))
     down = (((0,), (0,)), ((), ()))
     dot = functools.partial(lax.dot_general, preferred_element_type=f32)
 
-    def scatter_fsdp(value):
-        return lax.psum_scatter(value, "fsdp", scatter_dimension=0, tiled=True)
+    def scatter_fsdp(value, groups=None):
+        return lax.psum_scatter(
+            value, "fsdp", scatter_dimension=0, tiled=True, axis_index_groups=groups)
+
+    cores = [list(range(c, fs, 2)) for c in range(2)]
+
+    def pair_sum(value):
+        value = value.reshape(fs // 2, 2, -1, value.shape[1])
+        mine, other = by_core(value[:, 0], value[:, 1])
+        other = lax.ppermute(other, "fsdp", [(i, i ^ 1) for i in range(fs)])
+        total = mine.astype(f32) + other.astype(f32)
+        return total.astype(bf16).reshape(-1, value.shape[3])
 
     down_term = dot(activated, d_branch, down).astype(bf16)
     down_grad = scatter_fsdp(down_term)
-    mixed_all = jnp.concatenate(spread_seq(after(mixed, h2), n), axis=0)
-    branch = dot(after(activated, down_term), w_down, (((1,), (0,)), ((), ())))
+    lse = lse.transpose(0, 2, 1)
+    mixed_pieces = spread_seq(after(mixed, h2), n)
+    branch = dot(after(activated, (down_term, lse)), w_down, (((1,), (0,)), ((), ())))
     d_gate_up = feed_back(after(d_branch, branch), w_down, gate_up)
-    branch = collect_seq([branch[j * own : (j + 1) * own] for j in range(n)], n)
-    block_out = (residual + branch).astype(bf16)
-    gate_up_term = dot(h2, d_gate_up, down).astype(bf16)
-    gate_up_grad = scatter_fsdp(gate_up_term)
-    d_h2 = dot(after(d_gate_up, gate_up_term), w_gate_up, across)
-    d_h2 = scatter_seq([d_h2[j * own : (j + 1) * own] for j in range(n)], n)
+    branch_own = branch[:own]
+    branch = exchange_seq(
+        [branch_own]
+        + [branch[j * own : (j + 1) * own].astype(bf16) for j in range(1, n)], n)
+    gate_up_term = pair_dot(h2_turned, d_gate_up, fs, 5)
+    gate_up_grad = scatter_fsdp(gate_up_term, cores)
+    (d_h2,) = dot_scatter(after(d_gate_up, gate_up_term), w_gate_up, n, 3)
     gain_two_grad = jnp.sum(d_h2 * normed_two, axis=0)
     bias_two_grad = jnp.sum(d_h2, axis=0)
     d_residual = d_own.astype(f32) + norm_back(d_h2, normed_two, inverse_two, gain_two)
 
     d_attended = d_residual.astype(bf16)
-    d_mixed = by_core(*[dot(d_attended, item, across).astype(bf16) for item in w_out])
-    d_mixed = jnp.concatenate(d_mixed, axis=1)
-    d_mixed = jnp.concatenate(exchange_seq(column_parts(d_mixed), n), axis=0)
+    d_mixed = jnp.concatenate(
+        [dot(d_attended, item, across).astype(bf16) for item in w_out], axis=1
+    )
+    d_mixed = exchange(d_mixed, n, part, False, 2)
     d_projected = attend_back(
-        slot, query, key, value, d_mixed, lse.transpose(0, 2, 1), tables
-    )
-    d_attended_part = exchange_seq(column_parts(after(d_attended, d_mixed)), n)
-    d_attended_part = jnp.concatenate(d_attended_part, axis=0)
+        slot, query, key, value, d_mixed, lse, tables
+    )
     down_pieces = spread_seq(after(down_grad, d_mixed), n)
+    qkv_term = pair_dot(h1_turned, d_projected, fs, 6)
+    qkv_grad = scatter_fsdp(qkv_term, cores)
+    d_h1, d_attended_part = dot_scatter(after(d_projected, qkv_term), w_first, n, 4, d_attended)
+    mixed_all = jnp.concatenate([after(item, d_h1) for item in mixed_pieces], axis=0)
     out_term = dot(mixed_all, d_attended_part, down).astype(bf16)
-    qkv_term = dot(h1, d_projected, down).astype(bf16)
-    qkv_grad = scatter_fsdp(qkv_term)
-    qkv_bias_part = jnp.sum(d_projected.astype(f32), axis=0)
-    d_h1 = dot(after(d_projected, qkv_term), w_qkv, across)
-    d_h1 = scatter_seq([d_h1[j * own : (j + 1) * own] for j in range(n)], n)
+    out_term = jnp.concatenate(by_core(out_term[:half], out_term[half:]), axis=0)
+    d_h1_first, d_h1 = d_h1, after(d_h1, out_term)
+    qkv_bias_part = jnp.sum(after(d_projected, d_h1).astype(f32), axis=0)
     gain_one_grad = jnp.sum(d_h1 * normed_one, axis=0)
     bias_one_grad = jnp.sum(d_h1, axis=0)
-    input_grad = (
-        d_residual + norm_back(d_h1, normed_one, inverse_one, gain_one)
-    ).astype(bf16)
-
+
+    branch = [branch_own] + [after(item, d_h1) for item in branch[1:]]
+    block_out = (residual + sum(item.astype(f32) for item in branch)).astype(bf16)
     bias_all = jnp.concatenate(
         [jnp.where(s == i, qkv_bias_part.reshape(3, part), 0.0) for i in range(n)], axis=1
     )
@@ -583,18 +898,23 @@
     small.append(jnp.zeros((fs, extra * part - 7 * rows), f32))
     small = jnp.concatenate(small, axis=1).astype(bf16).reshape(fs, extra, part)
     out_term = jnp.concatenate([out_term.reshape(fs, rows, part), small], axis=1)
-    out_grad = scatter_fsdp(out_term.reshape(fs * (rows + extra), part))
+    out_term = out_term.reshape(fs * (rows + extra), part)
+    out_term = pair_sum(out_term)
+    out_grad = scatter_fsdp(out_term, cores)
+    input_grad = (
+        d_residual + norm_back(after(d_h1, out_term), normed_one, inverse_one, gain_one)
+    ).astype(bf16)
 
     down_total = jnp.stack(natural(down_pieces)).reshape(shard, width).astype(f32)
-    gate_up_pieces = gather_streams(after(gate_up_grad, qkv_term), n, d_h1)
+    gate_up_pieces = gather_streams(after(gate_up_grad, d_projected), n, d_h1_first)
     gate_total, up_total = finish(
         s, gate_up_pieces, (ffn, ffn),
         functools.partial(place_units, fs), min(64, rows // 2))
-    qkv_pieces = gather_streams(after(qkv_grad, gate_up_pieces[0][n - 1]), n)
+    qkv_pieces = gather_streams(after(qkv_grad, d_h1_first), n)
     (qkv_total,) = finish(
         s, qkv_pieces, (3 * width,),
         functools.partial(place_columns, 3), min(64, rows // 2))
-    out_pieces = spread_seq(after(out_grad, qkv_pieces[1][n - 1]), n)
+    out_pieces = spread_seq(out_grad, n)
     (out_total,) = finish(
         s, [out_pieces], (width,),
         functools.partial(place_columns, 1), rows, rows)

time: 793 us -> 912 us (1.15)
  Pallas kernels: 102 us -> 289 us
  matrix products: 128 us -> 64.5 us
  waiting for transfers between devices: 362 us -> 380 us
  starting transfers between devices: 66.3 us -> 50.9 us
  other arithmetic: 63.4 us -> 51.1 us
    pallas_call x0 -> x7, Pallas kernels: none -> 187 us  [the longest x2 104 us: dot_scatter(): pl.pallas_call(functools.partial(dot_scatter_kernel, n=n, tile=tile, ride...]
    reduce_scatter x4, waiting for transfers between devices: 0.03 us -> 181 us  [scatter_fsdp(): lax.psum_scatter(value, 'fsdp', scatter_dimension=0, tiled=True, axis_ind...]
    ppermute x63 -> x42, waiting for transfers between devices: 356 us -> 194 us  [swap(): return lax.ppermute(value, 'seq', [(i, i ^ mask) for i in range(n)])]
    dot_general x8 -> x3, matrix products: 92.7 us -> 19.8 us  [the longest x1 12.2 us: body(): dot(after(activated, (down_term, lse)), w_down, (((1,), (0,)), ((), ())))]
    ppermute x63 -> x42, starting transfers between devices: 66 us -> 50.6 us  [swap(): return lax.ppermute(value, 'seq', [(i, i ^ mask) for i in range(n)])]
    dot_general x1, matrix products: 6.08 us -> 16.3 us  [body(): jnp.dot(gate_weight, pick, preferred_element_type=f32).astype(bf16)]
  transfers between devices with their start and end apart: 71 -> 51, of which waited for: 36 -> 22; matrix products, arithmetic and copies ran while one was open for 23% -> 14% of each run, Pallas kernels for 11% -> 31%
where the time goes in v2:
time: 912 us; the launch traced here: 899 us
  waiting for transfers between devices  380 us (42%)
  Pallas kernels  289 us (32%)
  matrix products  64.5 us (7%)
  other arithmetic  51.1 us (6%)
  starting transfers between devices  50.9 us (6%)
  local copies, waits for them, and re-layouts  31.4 us (3%)
  blocking collectives  15.9 us (2%)
  between operations  15.4 us (2%)
    ppermute x42, waiting for transfers between devices, swap(): return lax.ppermute(value, 'seq', [(i, i ^ mask) for i in range(n)])  194 us
    reduce_scatter x4, waiting for transfers between devices, scatter_fsdp(): lax.psum_scatter(value, 'fsdp', scatter_dimension=0, tiled=True, axis_ind...  181 us
    pallas_call x2, Pallas kernels, dot_scatter(): pl.pallas_call(functools.partial(dot_scatter_kernel, n=n, tile=tile, ride...  104 us
    ppermute x42, starting transfers between devices, swap(): return lax.ppermute(value, 'seq', [(i, i ^ mask) for i in range(n)])  50.6 us
    pallas_call x2, Pallas kernels, pair_dot(): pl.pallas_call(functools.partial(pair_dot_kernel, shards=shards, tile=til...  37.6 us
    pallas_call x2, Pallas kernels, exchange(): pl.pallas_call(functools.partial(exchange_kernel, n=n, part=part, to_colu...  33.9 us
    pallas_call x1, Pallas kernels, attend_back(): pl.pallas_call(functools.partial(attend_back_kernel, tile=tile), grid_spe...  26.4 us
    pallas_call x1, Pallas kernels, attend(): pl.pallas_call(functools.partial(attend_kernel, tile=tile), grid_spec=plt...  23.9 us
  transfers between devices with their start and end apart: 51, of which 22 were waited for; matrix products, arithmetic and copies ran while one was open for 14% of the time, Pallas kernels for 31%

profile of v2, /device:TPU:0, one launch (start us, length us, event | category | flops | bytes accessed | tf_op | source)
XLA Modules:
  0.0 899.1 jit_solution(15595612745336245716)
XLA Ops:
  12.2 15.9 %all-gather.1 = bf16[8,1,1792]{2,1,0:T(2,128)(2,1)S(1)} all-gather(bf16[1,1,1792]{2,1,0:T(2,128)(2,1)S(1)} %reshape.248), channel_id=2, replica_groups=mesh['seq'=4,'fsdp'=8] {'fsdp'}, dimensions={0}, use_global_device_ids=true | all-gather | bytes 32256 | tf_op jit(solution)/shard_map/all_gather | solution.py:766
  39.0 16.3 %fusion.27 = bf16[256,1408]{1,0:T(8,128)(2,1)S(1)} fusion(bf16[256,5632]{1,0:T(8,128)(2,1)S(1)} %copy-done.33, s32[1408]{0:T(1024)S(1)} %fusion.62), kind=kOutput, calls=%fused_computation.34 | convolution fusion | flops 4068376576 | bytes 3610112 | tf_op jit(solution)/shard_map/dot_general | solution.py:795
  60.9 11.4 %collective-permute-done.1 = bf16[128,2048]{1,0:T(8,128)(2,1)S(1)} collective-permute-done((bf16[128,2048]{1,0:T(8,128)(2,1)}, bf16[128,2048]{1,0:T(8,128)(2,1)S(1)}, u32[]{:S(2)}, u32[]{:S(2)}) %collective-permute-start.1) | collective-permute-done | bytes 524320 | tf_op jit(solution)/shard_map/ppermute | solution.py:38
  105.2 22.5 %collective-permute-done.8 = bf16[1024,512]{1,0:T(8,128)(2,1)S(1)} collective-permute-done((bf16[1024,512]{1,0:T(8,128)(2,1)S(1)}, bf16[1024,512]{1,0:T(8,128)(2,1)S(1)}, u32[]{:S(2)}, u32[]{:S(2)}) %collective-permute-start.8) | collective-permute-done | bytes 1048608 | tf_op jit(solution)/shard_map/ppermute | solution.py:38
  127.7 19.3 %collective-permute-done.7 = bf16[1024,512]{1,0:T(8,128)(2,1)S(1)} collective-permute-done((bf16[1024,512]{1,0:T(8,128)(2,1)S(1)}, bf16[1024,512]{1,0:T(8,128)(2,1)S(1)}, u32[]{:S(2)}, u32[]{:S(2)}) %collective-permute-start.7) | collective-permute-done | bytes 1048608 | tf_op jit(solution)/shard_map/ppermute | solution.py:38
  161.1 12.0 %project.1 = (f32[1024,1536]{1,0:T(8,128)}, bf16[2048,1024]{1,0:T(8,128)(2,1)}) custom-call(bf16[1024,2048]{1,0:T(8,128)(2,1)} %constant_dynamic-update-slice_fusion.h_ref, bf16[2048,2048]{1,0:T(8,128)(2,1)} %all-gather.6.cloned.1.call-done.w_ref, f32[1,1536]{1,0:T(1,128)} %bitcast.140), custom_call_target="tpu_custom_call" | custom-call | flops 6442450944 | bytes 20971520 | tf_op jit(solution)/shard_map/project/pallas_call | solution.py:554
  173.1 23.9 %attend.1 = (bf16[1024,512]{1,0:T(8,128)(2,1)}, f32[4,1024,2]{2,1,0:T(8,128)}, bf16[1024,512]{1,0:T(8,128)(2,1)}, bf16[1024,512]{1,0:T(8,128)(2,1)}, bf16[1024,512]{1,0:T(8,128)(2,1)}) custom-call(s32[8]{0:T(128)} %select_reduce_fusion.slot_ref, f32[1024,1536]{1,0:T(8,128)} %get-tuple-element.60.q_ref.k_ref.v_ref, ...), custom_call_target="tpu_custom_call" | custom-call | flops 2147483648 | bytes 12582912 | tf_op jit(solution)/shard_map/attend/pallas_call | solution.py:441
  197.0 16.7 %shard_map.220 = bf16[256,2048]{1,0:T(8,128)(2,1)} custom-call(bf16[1024,512]{1,0:T(8,128)(2,1)} %get-tuple-element.61.x_ref), custom_call_target="tpu_custom_call" | custom-call | bytes 15728640 | tf_op jit(solution)/shard_map/pallas_call | solution.py:370
  266.6 19.7 %feed.1 = (f32[1024,2816]{1,0:T(8,128)}, bf16[1024,1408]{1,0:T(8,128)(2,1)}, bf16[2048,1024]{1,0:T(8,128)(2,1)}) custom-call(bf16[1024,2048]{1,0:T(8,128)(2,1)} %constant_dynamic-update-slice_fusion.7.h_ref, bf16[2048,2816]{1,0:T(8,128)(2,1)} %all-gather.8.cloned.1.call-done.w_ref), custom_call_target="tpu_custom_call" | custom-call | flops 11811160064 | bytes 34340864 | tf_op jit(solution)/shard_map/feed/pallas_call | solution.py:589
  296.8 12.2 %fusion.85 = (bf16[1024,2048]{1,0:T(8,128)(2,1)}, f32[1024,2048]{1,0:T(8,128)}) fusion(bf16[1024,1408]{1,0:T(8,128)(2,1)} %get-tuple-element.68, bf16[1408,2048]{1,0:T(8,128)(2,1)} %all-gather.10.cloned.1.call-done.w_ref), kind=kOutput, calls=%fused_computation.190 | convolution fusion | flops 5907677184 | bytes 21233664 | tf_op jit(solution)/shard_map/dot_general | solution.py:851
  309.0 14.2 %feed_back.1.b_ref.a_ref = bf16[1024,2816]{1,0:T(8,128)(2,1)} custom-call(bf16[1024,2048]{1,0:T(8,128)(2,1)} %pad_maximum_fusion.1.d_ref, bf16[1408,2048]{1,0:T(8,128)(2,1)} %all-gather.10.cloned.1.call-done.w_ref, f32[1024,2816]{1,0:T(8,128)} %get-tuple-element.73.both_ref), custom_call_target="tpu_custom_call" | custom-call | flops 5905580032 | bytes 27262976 | tf_op jit(solution)/shard_map/feed_back/pallas_call | solution.py:628
  323.2 23.1 %shard_map.221 = bf16[1024,2816]{1,0:T(8,128)(2,1)} custom-call(bf16[2048,1024]{1,0:T(8,128)(2,1)} %get-tuple-element.74.a_ref, bf16[1024,2816]{1,0:T(8,128)(2,1)} %feed_back.1.b_ref.a_ref), custom_call_target="tpu_custom_call" | custom-call | flops 11811160064 | bytes 28835840 | tf_op jit(solution)/shard_map/pallas_call | solution.py:307
  346.2 48.1 %shard_map.222 = f32[256,2048]{1,0:T(8,128)} custom-call(bf16[1024,2816]{1,0:T(8,128)(2,1)} %feed_back.1.b_ref.a_ref, bf16[2048,2816]{1,0:T(8,128)(2,1)} %all-gather.8.cloned.1.call-done.w_ref), custom_call_target="tpu_custom_call" | custom-call | flops 11811160064 | bytes 83886080 | tf_op jit(solution)/shard_map/pallas_call | solution.py:213
  409.3 17.2 %shard_map.223.d_ref = bf16[1024,512]{1,0:T(8,128)(2,1)} custom-call(bf16[256,2048]{1,0:T(8,128)(2,1)} %pad_maximum_fusion.7.x_ref), custom_call_target="tpu_custom_call" | custom-call | bytes 15728640 | tf_op jit(solution)/shard_map/pallas_call | solution.py:370
  426.5 26.4 %attend_back.1.b_ref.a_ref = bf16[1024,1536]{1,0:T(8,128)(2,1)} custom-call(s32[8]{0:T(128)} %select_reduce_fusion.slot_ref, bf16[1024,512]{1,0:T(8,128)(2,1)} %get-tuple-element.69.q_ref, bf16[1024,512]{1,0:T(8,128)(2,1)} %get-tuple-element.70.k_ref, bf16[1024,512]{1,0:T(8,128)(2,1)} %get-tuple-element.71.v_ref, bf16[1024,512]{1,0:T(8,128)(2,1)} %shard_map.223.d_ref, ...), custom_call_target="tpu_custom_call" | custom-call | flops 5368709120 | bytes 8388608 | tf_op jit(solution)/shard_map/attend_back/pallas_call | solution.py:524
  452.9 14.5 %shard_map.224 = bf16[1024,1536]{1,0:T(8,128)(2,1)} custom-call(bf16[2048,1024]{1,0:T(8,128)(2,1)} %get-tuple-element.76.a_ref, bf16[1024,1536]{1,0:T(8,128)(2,1)} %attend_back.1.b_ref.a_ref), custom_call_target="tpu_custom_call" | custom-call | flops 6442450944 | bytes 15728640 | tf_op jit(solution)/shard_map/pallas_call | solution.py:307
  467.4 55.4 %shard_map.225 = (f32[256,2048]{1,0:T(8,128)}, bf16[1024,512]{1,0:T(8,128)(2,1)}) custom-call(bf16[1024,1536]{1,0:T(8,128)(2,1)} %attend_back.1.b_ref.a_ref, bf16[2048,2048]{1,0:T(8,128)(2,1)} %all-gather.6.cloned.1.call-done.w_ref, bf16[256,2048]{1,0:T(8,128)(2,1)} %copy-done.15), custom_call_target="tpu_custom_call" | custom-call | flops 6442450944 | bytes 83886080 | tf_op jit(solution)/shard_map/pallas_call | solution.py:213
  547.4 23.5 %collective-permute-done.24 = bf16[256,2048]{1,0:T(8,128)(2,1)S(1)} collective-permute-done((bf16[256,2048]{1,0:T(8,128)(2,1)S(1)}, bf16[256,2048]{1,0:T(8,128)(2,1)S(1)}, u32[]{:S(2)}, u32[]{:S(2)}) %collective-permute-start.24) | collective-permute-done | bytes 1048608 | tf_op jit(solution)/shard_map/ppermute | solution.py:38
  570.8 21.6 %collective-permute-done.23 = bf16[256,2048]{1,0:T(8,128)(2,1)S(1)} collective-permute-done((bf16[256,2048]{1,0:T(8,128)(2,1)S(1)}, bf16[256,2048]{1,0:T(8,128)(2,1)S(1)}, u32[]{:S(2)}, u32[]{:S(2)}) %collective-permute-start.23) | collective-permute-done | bytes 1048608 | tf_op jit(solution)/shard_map/ppermute | solution.py:38
  599.4 29.8 %reduce-scatter.7.cloned.1.call-done = bf16[256,1536]{1,0:T(8,128)(2,1)} async-done(((bf16[1024,1536]{1,0:T(8,128)(2,1)}), bf16[256,1536]{1,0:T(8,128)(2,1)}) %reduce-scatter.7.cloned.1.call-update) | async-done | bytes 786448 | tf_op jit(solution)/shard_map/reduce_scatter | solution.py:835
  644.5 89.0 %reduce-scatter.9.cloned.1.call-done = bf16[256,2816]{1,0:T(8,128)(2,1)} async-done(((bf16[1024,2816]{1,0:T(8,128)(2,1)}), bf16[256,2816]{1,0:T(8,128)(2,1)}) %reduce-scatter.9.cloned.1.call-update) | async-done | bytes 1441808 | tf_op jit(solution)/shard_map/reduce_scatter | solution.py:835
  739.0 62.7 %reduce-scatter.11.cloned.1.call-done = bf16[176,2048]{1,0:T(8,128)(2,1)} async-done(((bf16[1408,2048]{1,0:T(8,128)(2,1)}), bf16[176,2048]{1,0:T(8,128)(2,1)}) %reduce-scatter.11.cloned.1.call-update) | async-done | bytes 720912 | tf_op jit(solution)/shard_map/reduce_scatter | solution.py:835
  822.9 27.3 %collective-permute-done.38.refs_6_ = bf16[128,2816]{1,0:T(8,128)(2,1)} collective-permute-done((bf16[128,2816]{1,0:T(8,128)(2,1)}, bf16[128,2816]{1,0:T(8,128)(2,1)}, u32[]{:S(2)}, u32[]{:S(2)}) %collective-permute-start.38) | collective-permute-done | bytes 720928 | tf_op jit(solution)/shard_map/ppermute | solution.py:38
  869.5 11.3 %collective-permute-done.40.refs_7_ = bf16[128,2816]{1,0:T(8,128)(2,1)} collective-permute-done((bf16[128,2816]{1,0:T(8,128)(2,1)}, bf16[128,2816]{1,0:T(8,128)(2,1)}, u32[]{:S(2)}, u32[]{:S(2)}) %collective-permute-start.40) | collective-permute-done | bytes 720928 | tf_op jit(solution)/shard_map/ppermute | solution.py:38
  (281 shorter events, 249.7 us)
Async XLA Ops:
  7.2 92.7 %all-gather.6.cloned.1.call-start = ((), (), s32[]{:S(2)}) async-start(), calls=%async_computation.4 | async-start | bytes 9437184 | tf_op jit(solution)/shard_map/all_gather | solution.py:763
  11.2 255.4 %all-gather.8.cloned.1.call-start = ((), (), s32[]{:S(2)}) async-start(), calls=%async_computation.5 | async-start | bytes 12976128 | tf_op jit(solution)/shard_map/all_gather | solution.py:763
  56.6 240.2 %all-gather.10.cloned.1.call-start = ((), (), s32[]{:S(2)}) async-start(), calls=%async_computation.6 | async-start | bytes 6488064 | tf_op jit(solution)/shard_map/all_gather | solution.py:763
  151.6 62.1 %collective-permute-start.9 = (bf16[1024,2048]{1,0:T(8,128)(2,1)}, bf16[1024,2048]{1,0:T(8,128)(2,1)}, u32[]{:S(2)}, u32[]{:S(2)}) collective-permute-start(bf16[1024,2048]{1,0:T(8,128)(2,1)} %pad_maximum_fusion), channel_id=1, source_target_pairs={{0,1},{1,0},{2,3},{3,2},{4,5},{5,4},{6,7},{7,6},{8,9},{9,8},{10,11... | collective-permute-start | bytes 12582920 | tf_op jit(solution)/shard_map/ppermute | solution.py:819
  151.6 88.2 %collective-permute-start.18 = (bf16[256,2048]{1,0:T(8,128)(2,1)}, bf16[256,2048]{1,0:T(8,128)(2,1)}, u32[]{:S(2)}, u32[]{:S(2)}) collective-permute-start(bf16[256,2048]{1,0:T(8,128)(2,1)} %bitcast.3), channel_id=1, source_target_pairs={{0,24},{8,16},{16,8},{24,0},{1,25},{9,17},{17,9},{25,1},{2,26},{10... | collective-permute-start | bytes 3145736 | tf_op jit(solution)/shard_map/ppermute | solution.py:38
  153.4 86.4 %collective-permute-start.17 = (bf16[256,2048]{1,0:T(8,128)(2,1)}, bf16[256,2048]{1,0:T(8,128)(2,1)}, u32[]{:S(2)}, u32[]{:S(2)}) collective-permute-start(bf16[256,2048]{1,0:T(8,128)(2,1)} %bitcast.3), channel_id=1, source_target_pairs={{0,16},{8,24},{16,0},{24,8},{1,17},{9,25},{17,1},{25,9},{2,18},{10... | collective-permute-start | bytes 3145736 | tf_op jit(solution)/shard_map/ppermute | solution.py:38
  153.8 86.0 %collective-permute-start.16 = (bf16[256,2048]{1,0:T(8,128)(2,1)}, bf16[256,2048]{1,0:T(8,128)(2,1)}, u32[]{:S(2)}, u32[]{:S(2)}) collective-permute-start(bf16[256,2048]{1,0:T(8,128)(2,1)} %bitcast.3), channel_id=1, source_target_pairs={{0,8},{8,0},{16,24},{24,16},{1,9},{9,1},{17,25},{25,17},{2,10},{10... | collective-permute-start | bytes 3145736 | tf_op jit(solution)/shard_map/ppermute | solution.py:38
  156.2 440.2 %reduce-scatter.5.cloned.1.call-start = ((), (), s32[]{:S(2)}) async-start(), calls=%async_computation.7 | async-start | bytes 1392640 | tf_op jit(solution)/shard_map/reduce_scatter | solution.py:835
  263.1 259.7 %collective-permute-start.22 = (bf16[256,2048]{1,0:T(8,128)(2,1)}, bf16[256,2048]{1,0:T(8,128)(2,1)}, u32[]{:S(2)}, u32[]{:S(2)}) collective-permute-start(bf16[256,2048]{1,0:T(8,128)(2,1)} %shard_map.220), channel_id=1, source_target_pairs={{0,24},{8,16},{16,8},{24,0},{1,25},{9,17},{17,9},{25,1},{2,26},{10... | collective-permute-start | bytes 3145736 | tf_op jit(solution)/shard_map/ppermute | solution.py:38
  264.6 258.3 %collective-permute-start.21 = (bf16[256,2048]{1,0:T(8,128)(2,1)}, bf16[256,2048]{1,0:T(8,128)(2,1)}, u32[]{:S(2)}, u32[]{:S(2)}) collective-permute-start(bf16[256,2048]{1,0:T(8,128)(2,1)} %shard_map.220), channel_id=1, source_target_pairs={{0,16},{8,24},{16,0},{24,8},{1,17},{9,25},{17,1},{25,9},{2,18},{10... | collective-permute-start | bytes 3145736 | tf_op jit(solution)/shard_map/ppermute | solution.py:38
  266.4 256.6 %collective-permute-start.20 = (bf16[256,2048]{1,0:T(8,128)(2,1)}, bf16[256,2048]{1,0:T(8,128)(2,1)}, u32[]{:S(2)}, u32[]{:S(2)}) collective-permute-start(bf16[256,2048]{1,0:T(8,128)(2,1)} %shard_map.220), channel_id=1, source_target_pairs={{0,8},{8,0},{16,24},{24,16},{1,9},{9,1},{17,25},{25,17},{2,10},{10... | collective-permute-start | bytes 3145736 | tf_op jit(solution)/shard_map/ppermute | solution.py:38
  539.6 89.5 %reduce-scatter.7.cloned.1.call-start = ((), (), s32[]{:S(2)}) async-start(), calls=%async_computation.8 | async-start | bytes 3932160 | tf_op jit(solution)/shard_map/reduce_scatter | solution.py:835
  540.2 193.3 %reduce-scatter.9.cloned.1.call-start = ((), (), s32[]{:S(2)}) async-start(), calls=%async_computation.9 | async-start | bytes 7208960 | tf_op jit(solution)/shard_map/reduce_scatter | solution.py:835
  540.8 260.9 %reduce-scatter.11.cloned.1.call-start = ((), (), s32[]{:S(2)}) async-start(), calls=%async_computation.10 | async-start | bytes 6488064 | tf_op jit(solution)/shard_map/reduce_scatter | solution.py:835
  596.4 137.1 %collective-permute-start.28 = (bf16[272,512]{1,0:T(8,128)(2,1)}, bf16[272,512]{1,0:T(8,128)(2,1)S(1)}, u32[]{:S(2)}, u32[]{:S(2)}) collective-permute-start(bf16[272,512]{1,0:T(8,128)(2,1)} %reduce-scatter.5.cloned.1.call-done.refs_0_), channel_id=1, source_target_pairs={{0,24},{8,16},{16,8},{24,0},{1,25},{9,17},{17,9},{25,1},{2,26},{10... | collective-permute-start | bytes 835592 | tf_op jit(solution)/shard_map/ppermute | solution.py:38
  598.0 137.0 %collective-permute-start.27 = (bf16[272,512]{1,0:T(8,128)(2,1)}, bf16[272,512]{1,0:T(8,128)(2,1)S(1)}, u32[]{:S(2)}, u32[]{:S(2)}) collective-permute-start(bf16[272,512]{1,0:T(8,128)(2,1)} %reduce-scatter.5.cloned.1.call-done.refs_0_), channel_id=1, source_target_pairs={{0,16},{8,24},{16,0},{24,8},{1,17},{9,25},{17,1},{25,9},{2,18},{10... | collective-permute-start | bytes 835592 | tf_op jit(solution)/shard_map/ppermute | solution.py:38
  633.3 168.4 %collective-permute-start.26 = (bf16[272,512]{1,0:T(8,128)(2,1)}, bf16[272,512]{1,0:T(8,128)(2,1)}, u32[]{:S(2)}, u32[]{:S(2)}) collective-permute-start(bf16[272,512]{1,0:T(8,128)(2,1)} %reduce-scatter.5.cloned.1.call-done.refs_0_), channel_id=1, source_target_pairs={{0,8},{8,0},{16,24},{24,16},{1,9},{9,1},{17,25},{25,17},{2,10},{10... | collective-permute-start | bytes 835592 | tf_op jit(solution)/shard_map/ppermute | solution.py:38
  640.8 162.3 %collective-permute-start.33 = (bf16[128,1536]{1,0:T(8,128)(2,1)S(1)}, bf16[128,1536]{1,0:T(8,128)(2,1)}, u32[]{:S(2)}, u32[]{:S(2)}) collective-permute-start(bf16[128,1536]{1,0:T(8,128)(2,1)S(1)} %get-tuple-element.93.refs_4_), channel_id=1, source_target_pairs={{0,8},{8,0},{16,24},{24,16},{1,9},{9,1},{17,25},{25,17},{2,10},{10... | collective-permute-start | bytes 1179656 | tf_op jit(solution)/shard_map/ppermute | solution.py:38
  644.0 161.3 %collective-permute-start.30 = (bf16[128,1536]{1,0:T(8,128)(2,1)S(1)}, bf16[128,1536]{1,0:T(8,128)(2,1)}, u32[]{:S(2)}, u32[]{:S(2)}) collective-permute-start(bf16[128,1536]{1,0:T(8,128)(2,1)S(1)} %get-tuple-element.92.refs_0_), channel_id=1, source_target_pairs={{0,16},{8,24},{16,0},{24,8},{1,17},{9,25},{17,1},{25,9},{2,18},{10... | collective-permute-start | bytes 1179656 | tf_op jit(solution)/shard_map/ppermute | solution.py:38
  733.5 71.2 %collective-permute-start.34 = (bf16[128,1536]{1,0:T(8,128)(2,1)S(1)}, bf16[128,1536]{1,0:T(8,128)(2,1)}, u32[]{:S(2)}, u32[]{:S(2)}) collective-permute-start(bf16[128,1536]{1,0:T(8,128)(2,1)S(1)} %collective-permute-done.32.refs_6_), channel_id=1, source_target_pairs={{0,8},{8,0},{16,24},{24,16},{1,9},{9,1},{17,25},{25,17},{2,10},{10... | collective-permute-start | bytes 1179656 | tf_op jit(solution)/shard_map/ppermute | solution.py:38
  735.0 71.7 %collective-permute-start.31 = (bf16[128,1536]{1,0:T(8,128)(2,1)}, bf16[128,1536]{1,0:T(8,128)(2,1)}, u32[]{:S(2)}, u32[]{:S(2)}) collective-permute-start(bf16[128,1536]{1,0:T(8,128)(2,1)} %collective-permute-done.29.refs_1_), channel_id=1, source_target_pairs={{0,16},{8,24},{16,0},{24,8},{1,17},{9,25},{17,1},{25,9},{2,18},{10... | collective-permute-start | bytes 1179656 | tf_op jit(solution)/shard_map/ppermute | solution.py:38
  801.7 50.5 %collective-permute-start.43 = (bf16[176,2048]{1,0:T(8,128)(2,1)}, bf16[176,2048]{1,0:T(8,128)(2,1)S(1)}, u32[]{:S(2)}, u32[]{:S(2)}) collective-permute-start(bf16[176,2048]{1,0:T(8,128)(2,1)} %reduce-scatter.11.cloned.1.call-done), channel_id=1, source_target_pairs={{0,8},{8,0},{16,24},{24,16},{1,9},{9,1},{17,25},{25,17},{2,10},{10... | collective-permute-start | bytes 2162696 | tf_op jit(solution)/shard_map/ppermute | solution.py:38
  803.2 50.5 %collective-permute-start.42 = (bf16[176,2048]{1,0:T(8,128)(2,1)}, bf16[176,2048]{1,0:T(8,128)(2,1)}, u32[]{:S(2)}, u32[]{:S(2)}) collective-permute-start(bf16[176,2048]{1,0:T(8,128)(2,1)} %reduce-scatter.11.cloned.1.call-done), channel_id=1, source_target_pairs={{0,16},{8,24},{16,0},{24,8},{1,17},{9,25},{17,1},{25,9},{2,18},{10... | collective-permute-start | bytes 2162696 | tf_op jit(solution)/shard_map/ppermute | solution.py:38
  804.7 49.5 %collective-permute-start.41 = (bf16[176,2048]{1,0:T(8,128)(2,1)}, bf16[176,2048]{1,0:T(8,128)(2,1)}, u32[]{:S(2)}, u32[]{:S(2)}) collective-permute-start(bf16[176,2048]{1,0:T(8,128)(2,1)} %reduce-scatter.11.cloned.1.call-done), channel_id=1, source_target_pairs={{0,24},{8,16},{16,8},{24,0},{1,25},{9,17},{17,9},{25,1},{2,26},{10... | collective-permute-start | bytes 2162696 | tf_op jit(solution)/shard_map/ppermute | solution.py:38
  (61 other events, 1844.8 us)
Sparse Core Ops, SparseCore 0:
  11.3 84.8 all-gather.5
  98.4 106.4 all-gather.7
  206.6 58.6 all-gather.9
  539.7 28.2 reduce-scatter.4
  570.2 58.9 reduce-scatter.6
  631.3 102.1 reduce-scatter.8
  736.4 65.2 reduce-scatter.10
